TPU v7x, 128 devices: a whole 4x4x4 slice. The times are simulated.
128 devices in a mesh: row: 16 (over y_hi, z, core), col: 8 (over y_lo, x).
Axes of the slice: x: 4, y: 4 (y_hi: 2, y_lo: 2; y = y_hi * 2 + y_lo), z: 4, core: 2. Of those that a mesh axis runs over, the one named last changes fastest.
Arguments:
- pair: bfloat16 [1024, 1024, 128], P('row', 'col'), may hold values from -6 to 6
- relpos: bfloat16 [128, 128], replicated, may hold values from -4 to 4
- pair_gain: float32 [128], replicated, may hold values from 0.1 to 1.9
- bias_weight: bfloat16 [128, 12], replicated, may hold values from -0.5 to 0.5
- single: float32 [1024, 384], P(('row', 'col')), may hold values from -6 to 6
- rotation_params: float32 [3, 1024], P(None, ('row', 'col')), may hold values from -4 to 4
- translation: float32 [3, 1024], P(None, ('row', 'col')), may hold values from -9 to 9
- residue_index: int32 [1024], P(('row', 'col')), may hold values from 0 to 203776, as said below
- residue_mask: int32 [1024], P(('row', 'col')), may hold values 0 or 1
- w_scalar: float32 [384, 576], replicated, may hold values from -0.3125 to 0.3125
- w_points: float32 [384, 576], replicated, may hold values from -0.3125 to 0.3125
- head_weights: float32 [12], replicated, may hold values from -2 to 1.5
- w_out: float32 [2112, 384], replicated, may hold values from -0.125 to 0.125
- w_hidden: float32 [384, 384], replicated, may hold values from -0.3125 to 0.3125
- w_back: float32 [384, 384], replicated, may hold values from -0.3125 to 0.3125
- w_frame: float32 [384, 6], replicated, may hold values from -0.078125 to 0.078125
Outputs:
- single_out: float32 [1024, 384], P(('row', 'col'))
- frames: float32 [12, 1024], P(None, ('row', 'col'))
Inputs may be any that keep to these rules, and one draw needn't show every extreme that they name: residue_index is strictly increasing along the crop, begins at 0 and ends at exactly 203776.
All inputs are finite; a program needn't handle non-finite values. No bound on the sum of `residue_mask` on one device may be relied on, other than what follows from the above.
Results may differ from a plain program's by a relative error of at most 0.0025.
Values may be sent and summed in bfloat16 or wider, within the bound.
A program may use at most 64 MiB of HBM per device.

v0:
```python
import math

import jax
import jax.numpy as jnp
from jax import lax
from jax.sharding import PartitionSpec as P

H = 12
C = 16
PQ = 4
PV = 8
BINS = 128
ITERS = 3


NORM_EPSILON = 1e-05
MASKED_LOGIT = -100000.0
NORM_FLOOR = 0.1
HIGHEST_PRECISION = lax.Precision.HIGHEST


def rows_first(arrays, axis, dims):
    turned = [jnp.moveaxis(a, dim, 0) for a, dim in zip(arrays, dims)]
    both = jnp.concatenate([t.reshape(len(t), -1) for t in turned], axis=1)
    whole, at, outs = (lax.all_gather(both, axis, axis=0, tiled=True), 0, [])
    for t, dim in zip(turned, dims):
        piece = whole[:, at : at + t[0].size].reshape(-1, *t.shape[1:])
        outs.append(jnp.moveaxis(piece, 0, dim))
        at += t[0].size
    return tuple(outs)


def in_order(parts, dim):
    shape = list(parts.shape[1:])
    shape[dim] *= parts.shape[0]
    return jnp.moveaxis(parts, 0, dim).reshape(shape)


def copy_for_each(value, axis):
    copies = jnp.broadcast_to(value, (lax.axis_size(axis), *value.shape))
    return lax.all_to_all(copies, axis, split_axis=0, concat_axis=0, tiled=True)


def gather_directly(value, axis, dim):
    return in_order(copy_for_each(value, axis), dim)


def broadcast(value, axis, root):
    return lax.dynamic_index_in_dim(lax.all_gather(value, axis), root, 0, keepdims=False)


def of_everyone(value, axis):
    return copy_for_each(value, axis).max(axis=0)


def sent_together(arrays, axis, dim, along):
    both = jnp.concatenate(arrays, axis=along)
    whole, at, outs = (lax.psum_scatter(both, axis, scatter_dimension=dim, tiled=True), 0, [])
    for a in arrays:
        outs.append(lax.slice_in_dim(whole, at, at + a.shape[along], axis=along))
        at += a.shape[along]
    return tuple(outs)


def layer_norm(values):
    center = values - jnp.mean(values, axis=-1, keepdims=True)
    spread = jnp.mean(center * center, axis=-1, keepdims=True)
    return center * lax.rsqrt(spread + NORM_EPSILON)


def rotation_from(update):
    quat_b, quat_c, quat_d = (update[0], update[1], update[2])
    inverse = 1.0 / (1.0 + quat_b * quat_b + quat_c * quat_c + quat_d * quat_d)
    entries = [
        1.0 + quat_b * quat_b - quat_c * quat_c - quat_d * quat_d,
        2.0 * (quat_b * quat_c - quat_d),
        2.0 * (quat_b * quat_d + quat_c),
        2.0 * (quat_b * quat_c + quat_d),
        1.0 - quat_b * quat_b + quat_c * quat_c - quat_d * quat_d,
        2.0 * (quat_c * quat_d - quat_b),
        2.0 * (quat_b * quat_d - quat_c),
        2.0 * (quat_c * quat_d + quat_b),
        1.0 - quat_b * quat_b - quat_c * quat_c + quat_d * quat_d,
    ]
    return jnp.stack(entries) * inverse


def to_global(rotation, points, translation):
    return jnp.stack(
        [
            rotation[3 * component] * points[0]
            + rotation[3 * component + 1] * points[1]
            + rotation[3 * component + 2] * points[2]
            + translation[component]
            for component in range(3)
        ]
    )


def to_local(rotation, points, translation):
    moved = [points[component] - translation[component] for component in range(3)]
    return jnp.stack(
        [
            rotation[component] * moved[0]
            + rotation[3 + component] * moved[1]
            + rotation[6 + component] * moved[2]
            for component in range(3)
        ]
    )


def compose(rotation, translation, update):
    turn = rotation_from(update[:3])
    new_rotation = jnp.stack(
        [
            rotation[3 * left] * turn[right]
            + rotation[3 * left + 1] * turn[3 + right]
            + rotation[3 * left + 2] * turn[6 + right]
            for left in range(3)
            for right in range(3)
        ]
    )
    new_translation = jnp.stack(
        [
            rotation[3 * left] * update[3]
            + rotation[3 * left + 1] * update[4]
            + rotation[3 * left + 2] * update[5]
            + translation[left]
            for left in range(3)
        ]
    )
    return (new_rotation, new_translation)


def project(single, rotation, translation, w_scalar, w_points):
    count = single.shape[0]
    scalars = jnp.dot(
        single, w_scalar, precision=HIGHEST_PRECISION, preferred_element_type=jnp.float32
    ).T
    scalars = scalars.reshape(3, H * C, count).astype(jnp.bfloat16)
    points = jnp.dot(
        single, w_points, precision=HIGHEST_PRECISION, preferred_element_type=jnp.float32
    ).T
    query_local = points[: 3 * H * PQ].reshape(3, H * PQ, count)
    key_local = points[3 * H * PQ : 6 * H * PQ].reshape(3, H * PQ, count)
    value_local = points[6 * H * PQ :].reshape(3, H * PV, count)
    return (
        scalars,
        to_global(rotation, query_local, translation),
        to_global(rotation, key_local, translation),
        to_global(rotation, value_local, translation),
    )


def advance(
    single, rotation, translation, scalar_out, point_out, pair_out, w_out, w_hidden, w_back, w_frame
):
    count = single.shape[0]
    local = to_local(rotation, point_out, translation)
    lengths = jnp.sqrt(jnp.sum(local * local, axis=0) + NORM_FLOOR)
    features = jnp.concatenate(
        [scalar_out, local.reshape(3 * H * PV, count), lengths, pair_out], axis=0
    )
    mixed = jnp.dot(
        features.T, w_out, precision=HIGHEST_PRECISION, preferred_element_type=jnp.float32
    )
    single = layer_norm(single + mixed)
    hidden = jax.nn.relu(
        jnp.dot(single, w_hidden, precision=HIGHEST_PRECISION, preferred_element_type=jnp.float32)
    )
    single = layer_norm(
        single
        + jnp.dot(hidden, w_back, precision=HIGHEST_PRECISION, preferred_element_type=jnp.float32)
    )
    update = jnp.dot(
        single, w_frame, precision=HIGHEST_PRECISION, preferred_element_type=jnp.float32
    ).T
    rotation, translation = compose(rotation, translation, update)
    return (single, rotation, translation)


def attend_block(
    query, keyval, query_side, key_side, value_side, bias, normed, pair_live, point_scale
):
    heads_query = query.reshape(H, C, -1)
    keys = keyval[0].reshape(H, C, -1)
    values = keyval[1].reshape(H, C, -1)
    query_grid = query_side.reshape(3, H, PQ, -1)
    key_grid = key_side.reshape(3, H, PQ, -1)
    value_grid = value_side.reshape(3, H, PV, -1)
    scores = jnp.einsum(
        "hci,hcj->hij", heads_query, keys, preferred_element_type=jnp.float32
    ) / math.sqrt(C)
    cross = jnp.einsum("ahpi,ahpj->hij", query_grid, key_grid, precision=HIGHEST_PRECISION)
    distance = (
        jnp.sum(query_grid * query_grid, axis=(0, 2))[:, :, None]
        + jnp.sum(key_grid * key_grid, axis=(0, 2))[:, None, :]
        - 2.0 * cross
    )
    logits = math.sqrt(1.0 / 3.0) * (scores + bias - point_scale[:, None, None] * distance)
    logits = jnp.where(pair_live[None], logits, MASKED_LOGIT)
    local_max = jnp.max(logits, axis=-1)
    unscaled = jnp.exp(logits - local_max[:, :, None])
    total_weight = jnp.sum(unscaled, axis=-1)
    rounded = unscaled.astype(jnp.bfloat16)
    scalar_sum = jnp.einsum("hij,hcj->hci", rounded, values, preferred_element_type=jnp.float32)
    point_sum = jnp.einsum("hij,ahpj->ahpi", unscaled, value_grid, precision=HIGHEST_PRECISION)
    pair_sum = jnp.einsum("hij,ijc->hci", rounded, normed, preferred_element_type=jnp.float32)
    return (local_max, total_weight, scalar_sum, point_sum, pair_sum)


def body(
    pair,
    relpos,
    pair_gain,
    bias_weight,
    single,
    rotation_params,
    translation,
    residue_index,
    residue_mask,
    w_scalar,
    w_points,
    head_weights,
    w_out,
    w_hidden,
    w_back,
    w_frame,
):
    row_rows = pair.shape[0]
    col_rows = pair.shape[1]
    owned = single.shape[0]
    row_place = lax.axis_index("row")
    col_place = lax.axis_index("col")
    index_all, mask_all = rows_first((residue_index, residue_mask), ("row", "col"), (0, 0))
    query_index = lax.dynamic_slice_in_dim(index_all, row_place * row_rows, row_rows, 0)
    key_index = lax.dynamic_slice_in_dim(index_all, col_place * col_rows, col_rows, 0)
    query_live = lax.dynamic_slice_in_dim(mask_all, row_place * row_rows, row_rows, 0) == 1
    key_live = lax.dynamic_slice_in_dim(mask_all, col_place * col_rows, col_rows, 0) == 1
    pair_live = query_live[:, None] & key_live[None, :]
    span_rows = math.gcd(row_rows, 64)

    def prepare(index):
        offset = (
            jnp.clip(key_index[None, :] - query_index[:, None], -(BINS // 2), BINS // 2 - 1)
            + BINS // 2
        )
        onehot = (offset[:, :, None] == lax.broadcasted_iota(jnp.int32, (1, 1, BINS), 2)).astype(
            jnp.bfloat16
        )
        embedded = jnp.dot(
            onehot.reshape(span_rows * col_rows, BINS), relpos, preferred_element_type=jnp.float32
        )
        summed = pair.astype(jnp.float32) + embedded.reshape(span_rows, col_rows, -1)
        normed_part = (layer_norm(summed) * pair_gain).astype(jnp.bfloat16)
        bias_part = jnp.einsum(
            "ijc,ch->hij", normed_part, bias_weight, preferred_element_type=jnp.float32
        )
        return (normed_part, bias_part)

    normed_blocks, bias_blocks = lax.map(
        prepare, jnp.arange(row_rows // span_rows, dtype=jnp.int32)
    )
    normed = normed_blocks.reshape(row_rows, col_rows, -1)
    bias = bias_blocks.transpose(1, 0, 2, 3).reshape(H, row_rows, col_rows)
    point_scale = jax.nn.softplus(head_weights) * (math.sqrt(2.0 / (9.0 * PQ)) / 2.0)
    rotation = rotation_from(rotation_params)
    state = single
    for step in range(ITERS):
        scalars, query_points, key_points, value_points = project(
            state, rotation, translation, w_scalar, w_points
        )
        query_flat = query_points.reshape(-1, owned)
        key_flat = key_points.reshape(-1, owned)
        value_flat = value_points.reshape(-1, owned)
        block_scalar = gather_directly(scalars, "col", 2)
        block_point = rows_first((query_flat, key_flat, value_flat), "col", (1, 1, 1))
        query = block_scalar[0]
        query_side = block_point[0]
        ratio = lax.axis_size("row") // lax.axis_size("col")
        scalar_pieces = []
        key_pieces = []
        value_pieces = []
        for part in range(ratio):
            root = col_place * ratio + part
            scalar_pieces.append(broadcast(block_scalar[1:], "row", root))
            key_piece, value_piece = (
                broadcast(block_point[1], "row", root),
                broadcast(block_point[2], "row", root),
            )
            key_pieces.append(key_piece)
            value_pieces.append(value_piece)
        keyval = jnp.concatenate(scalar_pieces, axis=2)
        key_side = jnp.concatenate(key_pieces, axis=1)
        value_side = jnp.concatenate(value_pieces, axis=1)
        local_max, total_weight, scalar_sum, point_sum, pair_sum = attend_block(
            query, keyval, query_side, key_side, value_side, bias, normed, pair_live, point_scale
        )
        pair_out = None
        row_top = of_everyone(local_max, "col")
        factor = jnp.exp(local_max - row_top)
        shares = sent_together(
            (
                total_weight * factor,
                (scalar_sum * factor[:, None, :]).reshape(H * C, row_rows),
                (point_sum * factor[None, :, None, :]).reshape(3 * H * PV, row_rows),
                (pair_sum * factor[:, None, :]).reshape(-1, row_rows),
            ),
            "col",
            1,
            0,
        )
        total = shares[0]
        scalar_out = (shares[1].reshape(H, C, owned) / total[:, None, :]).reshape(H * C, owned)
        point_out = (shares[2].reshape(3, H, PV, owned) / total[None, :, None, :]).reshape(
            3, H * PV, owned
        )
        pair_out = (shares[3].reshape(H, -1, owned) / total[:, None, :]).reshape(-1, owned)
        state, rotation, translation = advance(
            state,
            rotation,
            translation,
            scalar_out,
            point_out,
            pair_out,
            w_out,
            w_hidden,
            w_back,
            w_frame,
        )
    frames = jnp.concatenate([rotation, translation], axis=0)
    return (state, frames)


def solution(mesh):
    placed = (
        P("row", "col", None),
        P(),
        P(),
        P(),
        P(("row", "col"), None),
        P(None, ("row", "col")),
        P(None, ("row", "col")),
        P(("row", "col")),
        P(("row", "col")),
        P(),
        P(),
        P(),
        P(),
        P(),
        P(),
        P(),
    )
    return jax.shard_map(
        body,
        mesh=mesh,
        in_specs=placed,
        out_specs=(P(("row", "col"), None), P(None, ("row", "col"))),
        check_vma=False,
    )
```

profile of v0, /device:TPU:0, one launch (start us, length us, event | category | flops | bytes accessed | tf_op | source)
XLA Modules:
  0.0 859.4 jit_solution(4518014439812937433)
XLA Ops:
  7.2 2.2 convolution_convert_fusion.2
  10.1 5.4 all-to-all-start
  17.2 2.0 fusion.105
  21.4 29.0 %all_gather.87 = f32[64,576]{1,0:T(8,128)S(1)} all-gather(f32[8,576]{1,0:T(8,128)S(1)} %pad_maximum_fusion.9), channel_id=1, replica_groups=mesh['row'=16,'col'=8] {'col'}, dimensions={0}, use_global_device_ids=true | all-gather | bytes 165888 | tf_op jit(solution)/shard_map/all_gather | solution.py:25
  51.9 311.7 %all-gather.6 = s32[128,8,2]{1,2,0:T(2,128)S(1)} all-gather(s32[1,8,2]{1,2,0:T(2,128)S(1)} %add_bitcast_fusion.27), channel_id=1, replica_groups=mesh['row'=16,'col'=8] {'row','col'}, dimensions={0}, use_global_device_ids=true | all-gather | bytes 8256 | tf_op jit(solution)/shard_map/all_gather | solution.py:25
  363.9 4.1 copy.370
  368.1 3.8 fusion.95
  371.9 2.0 copy-done.2
  375.8 24.2 %all-gather.7 = f32[16,144,64]{1,2,0:T(8,128)} all-gather(f32[1,144,64]{1,2,0:T(8,128)} %get-tuple-element.84), channel_id=2, replica_groups=mesh['row'=16,'col'=8] {'row'}, dimensions={0}, use_global_device_ids=true | all-gather | bytes 626688 | tf_op jit(solution)/shard_map/all_gather | solution.py:49
  405.2 3.2 multiply_convert_fusion
  413.5 23.1 %all_gather.86 = bf16[16,2,192,64]{2,3,1,0:T(8,128)(2,1)S(1)} all-gather(bf16[1,2,192,64]{2,3,1,0:T(8,128)(2,1)S(1)} %slice_bitcast_fusion.11), channel_id=1, replica_groups=mesh['row'=16,'col'=8] {'row'}, dimensions={0}, use_global_device_ids=true | all-gather | bytes 835584 | tf_op jit(solution)/shard_map/all_gather | solution.py:49
  439.7 2.7 fusion.96
  443.1 3.3 all-to-all-start.1
  449.5 3.0 all-to-all-done.1
  457.0 2.8 fusion.2
  463.4 1.8 fusion.28
  465.5 2.1 concatenate.99
  467.6 33.0 %reduce-scatter.4.cloned.1.call-done = f32[2028,8]{0,1:T(8,128)} async-done(((f32[2028,64]{0,1:T(8,128)}), f32[2028,8]{0,1:T(8,128)}) %reduce-scatter.4.cloned.1.call-update) | async-done | bytes 64912 | tf_op jit(solution)/shard_map/reduce_scatter | solution.py:58
  505.0 1.8 fusion.97
  511.3 28.2 %all_gather.94 = f32[64,576]{1,0:T(8,128)S(1)} all-gather(f32[8,576]{1,0:T(8,128)S(1)} %pad_maximum_fusion.10), channel_id=1, replica_groups=mesh['row'=16,'col'=8] {'col'}, dimensions={0}, use_global_device_ids=true | all-gather | bytes 165888 | tf_op jit(solution)/shard_map/all_gather | solution.py:25
  541.7 3.4 all-to-all-start.2
  546.1 26.9 %all-gather.9 = f32[16,144,64]{1,2,0:T(8,128)S(1)} all-gather(f32[1,144,64]{1,2,0:T(8,128)S(1)} %get-tuple-element.82), channel_id=4, replica_groups=mesh['row'=16,'col'=8] {'row'}, dimensions={0}, use_global_device_ids=true | all-gather | bytes 626688 | tf_op jit(solution)/shard_map/all_gather | solution.py:49
  574.6 1.6 copy.465
  576.2 1.6 multiply_reduce_fusion.3
  578.5 22.4 %all_gather.93 = bf16[16,2,192,64]{2,3,1,0:T(8,128)(2,1)S(1)} all-gather(bf16[1,2,192,64]{2,3,1,0:T(8,128)(2,1)S(1)} %slice_bitcast_fusion.8), channel_id=1, replica_groups=mesh['row'=16,'col'=8] {'row'}, dimensions={0}, use_global_device_ids=true | all-gather | bytes 835584 | tf_op jit(solution)/shard_map/all_gather | solution.py:49
  603.8 2.7 fusion.99
  607.2 5.2 all-to-all-start.3
  612.7 1.9 fusion.36
  616.2 2.5 all-to-all-done.3
  624.6 2.8 fusion.3
  631.0 1.8 fusion.27
  633.0 2.1 concatenate.109
  635.1 35.0 %reduce-scatter.6.cloned.1.call-done = f32[2028,8]{0,1:T(8,128)} async-done(((f32[2028,64]{0,1:T(8,128)}), f32[2028,8]{0,1:T(8,128)}) %reduce-scatter.6.cloned.1.call-update) | async-done | bytes 64912 | tf_op jit(solution)/shard_map/reduce_scatter | solution.py:58
  675.2 2.6 fusion.100
  682.4 28.2 %all_gather.101 = f32[64,576]{1,0:T(8,128)S(1)} all-gather(f32[8,576]{1,0:T(8,128)S(1)} %pad_maximum_fusion.11), channel_id=1, replica_groups=mesh['row'=16,'col'=8] {'col'}, dimensions={0}, use_global_device_ids=true | all-gather | bytes 165888 | tf_op jit(solution)/shard_map/all_gather | solution.py:25
  712.8 3.4 all-to-all-start.4
  717.2 26.9 %all-gather.11 = f32[16,144,64]{1,2,0:T(8,128)S(1)} all-gather(f32[1,144,64]{1,2,0:T(8,128)S(1)} %get-tuple-element.80), channel_id=6, replica_groups=mesh['row'=16,'col'=8] {'row'}, dimensions={0}, use_global_device_ids=true | all-gather | bytes 626688 | tf_op jit(solution)/shard_map/all_gather | solution.py:49
  747.3 1.6 multiply_reduce_fusion.1
  749.6 22.4 %all_gather.100 = bf16[16,2,192,64]{2,3,1,0:T(8,128)(2,1)S(1)} all-gather(bf16[1,2,192,64]{2,3,1,0:T(8,128)(2,1)S(1)} %slice_bitcast_fusion.5), channel_id=1, replica_groups=mesh['row'=16,'col'=8] {'row'}, dimensions={0}, use_global_device_ids=true | all-gather | bytes 835584 | tf_op jit(solution)/shard_map/all_gather | solution.py:49
  774.9 2.7 fusion.102
  778.3 5.2 all-to-all-start.5
  783.8 1.9 fusion.38
  787.3 2.4 all-to-all-done.5
  795.7 2.8 fusion.4
  802.0 1.8 fusion.26
  804.0 2.1 concatenate.119
  806.2 35.0 %reduce-scatter.8.cloned.1.call-done = f32[2028,8]{0,1:T(8,128)} async-done(((f32[2028,64]{0,1:T(8,128)}), f32[2028,8]{0,1:T(8,128)}) %reduce-scatter.8.cloned.1.call-update) | async-done | bytes 64912 | tf_op jit(solution)/shard_map/reduce_scatter | solution.py:58
  846.1 2.5 fusion.103
  (520 shorter events, 102.3 us)
Async XLA Ops:
  7.2 497.7 %copy-start = (f32[2112,384]{1,0:T(8,128)S(1)}, f32[2112,384]{1,0:T(8,128)}, u32[]{:S(2)}) copy-start(f32[2112,384]{1,0:T(8,128)} %param.28) | copy-start | bytes 9732100
  7.2 44.7 %copy-start.105 = (s32[8]{0:T(128)S(1)}, s32[8]{0:T(128)}, u32[]{:S(2)}) copy-start(s32[8]{0:T(128)} %param.24) | copy-start | bytes 100
  7.2 44.7 %copy-start.106 = (s32[8]{0:T(128)S(1)}, s32[8]{0:T(128)}, u32[]{:S(2)}) copy-start(s32[8]{0:T(128)} %param.23) | copy-start | bytes 100
  10.1 402.7 %all-to-all-start = ((bf16[8,3,192,8]{2,3,1,0:T(8,128)(2,1)}), bf16[8,3,192,8]{2,3,1,0:T(8,128)(2,1)S(1)}, u32[]{:S(2)}, u32[]{:S(2)}) async-start(bf16[8,3,192,8]{2,3,1,0:T(8,128)(2,1)} %broadcast_in_dim.51), calls=%async_computation | async-start | bytes 196608 | tf_op jit(solution)/shard_map/all_to_all | solution.py:41
  15.6 445.1 %all-gather.17.cloned.1.call-start = ((), (), s32[]{:S(2)}) async-start(), calls=%async_computation.12 | async-start | bytes 1671168 | tf_op jit(solution)/shard_map/all_gather | solution.py:49
  19.2 348.8 %copy-start.28 = (bf16[128,128]{1,0:T(8,128)(2,1)S(1)}, bf16[128,128]{1,0:T(8,128)(2,1)}, u32[]{:S(2)}) copy-start(bf16[128,128]{1,0:T(8,128)(2,1)} %param.17) | copy-start | bytes 98308
  371.9 32.7 %copy-start.107 = (f32[12]{0:T(128)S(1)}, f32[12]{0:T(128)}, u32[]{:S(2)}) copy-start(f32[12]{0:T(128)} %param.27) | copy-start | bytes 148
  371.9 33.2 %copy-start.104 = (f32[128]{0:T(128)S(1)}, f32[128]{0:T(128)}, u32[]{:S(2)}) copy-start(f32[128]{0:T(128)} %param.18) | copy-start | bytes 1540
  375.8 36.5 %copy-start.13 = (f32[144,64]{1,0:T(8,128)}, f32[144,64]{1,0:T(8,128)S(1)}, u32[]{:S(2)}) copy-start(f32[144,64]{1,0:T(8,128)S(1)} %copy.377) | copy-start | bytes 110596
  443.1 9.5 %all-to-all-start.1 = ((f32[8,1,768]{2,1,0:T(1,128)}), f32[8,1,768]{2,1,0:T(1,128)S(1)}, u32[]{:S(2)}, u32[]{:S(2)}) async-start(f32[8,1,768]{2,1,0:T(1,128)} %reshape.2142), calls=%async_computation.1 | async-start | bytes 49152 | tf_op jit(solution)/shard_map/all_to_all | solution.py:41
  446.4 54.1 %reduce-scatter.4.cloned.1.call-start = ((), (), s32[]{:S(2)}) async-start(), calls=%async_computation.9 | async-start | bytes 589824 | tf_op jit(solution)/shard_map/reduce_scatter | solution.py:58
  465.2 37.5 %copy-start.75 = (f32[8]{0:T(128)S(1)}, f32[8]{0:T(128)}, u32[]{:S(2)}) copy-start(f32[8]{0:T(128)} %copy-done.74) | copy-start | bytes 100
  465.2 37.6 %copy-start.77 = (f32[8]{0:T(128)S(1)}, f32[8]{0:T(128)}, u32[]{:S(2)}) copy-start(f32[8]{0:T(128)} %copy-done.76) | copy-start | bytes 100
  465.2 37.6 %copy-start.79 = (f32[8]{0:T(128)S(1)}, f32[8]{0:T(128)}, u32[]{:S(2)}) copy-start(f32[8]{0:T(128)} %copy-done.78) | copy-start | bytes 100
  465.3 37.6 %copy-start.81 = (f32[8]{0:T(128)S(1)}, f32[8]{0:T(128)}, u32[]{:S(2)}) copy-start(f32[8]{0:T(128)} %copy-done.80) | copy-start | bytes 100
  465.3 37.6 %copy-start.83 = (f32[8]{0:T(128)S(1)}, f32[8]{0:T(128)}, u32[]{:S(2)}) copy-start(f32[8]{0:T(128)} %copy-done.82) | copy-start | bytes 100
  465.3 37.6 %copy-start.85 = (f32[8]{0:T(128)S(1)}, f32[8]{0:T(128)}, u32[]{:S(2)}) copy-start(f32[8]{0:T(128)} %copy-done.84) | copy-start | bytes 100
  465.3 37.6 %copy-start.87 = (f32[8]{0:T(128)S(1)}, f32[8]{0:T(128)}, u32[]{:S(2)}) copy-start(f32[8]{0:T(128)} %copy-done.86) | copy-start | bytes 100
  465.3 37.6 %copy-start.89 = (f32[8]{0:T(128)S(1)}, f32[8]{0:T(128)}, u32[]{:S(2)}) copy-start(f32[8]{0:T(128)} %copy-done.88) | copy-start | bytes 100
  465.3 37.6 %copy-start.91 = (f32[8]{0:T(128)S(1)}, f32[8]{0:T(128)}, u32[]{:S(2)}) copy-start(f32[8]{0:T(128)} %copy-done.90) | copy-start | bytes 100
  465.3 37.6 %copy-start.93 = (f32[8]{0:T(128)S(1)}, f32[8]{0:T(128)}, u32[]{:S(2)}) copy-start(f32[8]{0:T(128)} %copy-done.92) | copy-start | bytes 100
  465.3 37.6 %copy-start.95 = (f32[8]{0:T(128)S(1)}, f32[8]{0:T(128)}, u32[]{:S(2)}) copy-start(f32[8]{0:T(128)} %copy-done.94) | copy-start | bytes 100
  465.3 37.6 %copy-start.97 = (f32[8]{0:T(128)S(1)}, f32[8]{0:T(128)}, u32[]{:S(2)}) copy-start(f32[8]{0:T(128)} %copy-done.96) | copy-start | bytes 100
  465.3 39.6 %copy-start.24 = (f32[8,384]{1,0:T(8,128)S(1)}, f32[8,384]{1,0:T(8,128)}, u32[]{:S(2)}) copy-start(f32[8,384]{1,0:T(8,128)} %param.20) | copy-start | bytes 36868
  510.2 31.5 %copy-start.63 = (f32[1,8]{1,0:T(1,128)}, f32[1,8]{1,0:T(1,128)S(1)}, u32[]{:S(2)}) copy-start(f32[1,8]{1,0:T(1,128)S(1)} %get-tuple-element.125) | copy-start | bytes 100
  510.4 31.3 %copy-start.59 = (f32[1,8]{1,0:T(1,128)}, f32[1,8]{1,0:T(1,128)S(1)}, u32[]{:S(2)}) copy-start(f32[1,8]{1,0:T(1,128)S(1)} %get-tuple-element.117) | copy-start | bytes 100
  541.7 36.8 %all-to-all-start.2 = ((bf16[8,3,192,8]{2,3,1,0:T(8,128)(2,1)}), bf16[8,3,192,8]{2,3,1,0:T(8,128)(2,1)S(1)}, u32[]{:S(2)}, u32[]{:S(2)}) async-start(bf16[8,3,192,8]{2,3,1,0:T(8,128)(2,1)} %broadcast_in_dim.54), calls=%async_computation.3 | async-start | bytes 196608 | tf_op jit(solution)/shard_map/all_to_all | solution.py:41
  545.1 83.3 %all-gather.19.cloned.1.call-start = ((), (), s32[]{:S(2)}) async-start(), calls=%async_computation.13 | async-start | bytes 1671168 | tf_op jit(solution)/shard_map/all_gather | solution.py:49
  546.1 55.5 %copy-start.15 = (f32[144,64]{1,0:T(8,128)}, f32[144,64]{1,0:T(8,128)S(1)}, u32[]{:S(2)}) copy-start(f32[144,64]{1,0:T(8,128)S(1)} %copy.402) | copy-start | bytes 110596
  574.6 27.0 %copy-start.19 = (f32[1,144,64]{2,1,0:T(8,128)}, f32[1,144,64]{2,1,0:T(8,128)S(1)}, u32[]{:S(2)}) copy-start(f32[1,144,64]{2,1,0:T(8,128)S(1)} %copy.466) | copy-start | bytes 110596
  606.5 16.4 %copy-start.21 = (f32[12,64]{1,0:T(8,128)}, f32[12,64]{1,0:T(8,128)S(1)}, u32[]{:S(2)}) copy-start(f32[12,64]{1,0:T(8,128)S(1)} %get-tuple-element.229) | copy-start | bytes 9220
  607.2 11.5 %all-to-all-start.3 = ((f32[8,1,768]{2,1,0:T(1,128)}), f32[8,1,768]{2,1,0:T(1,128)S(1)}, u32[]{:S(2)}, u32[]{:S(2)}) async-start(f32[8,1,768]{2,1,0:T(1,128)} %reshape.2144), calls=%async_computation.4 | async-start | bytes 49152 | tf_op jit(solution)/shard_map/all_to_all | solution.py:41
  612.4 57.7 %reduce-scatter.6.cloned.1.call-start = ((), (), s32[]{:S(2)}) async-start(), calls=%async_computation.10 | async-start | bytes 589824 | tf_op jit(solution)/shard_map/reduce_scatter | solution.py:58
  681.3 31.5 %copy-start.69 = (f32[1,8]{1,0:T(1,128)}, f32[1,8]{1,0:T(1,128)S(1)}, u32[]{:S(2)}) copy-start(f32[1,8]{1,0:T(1,128)S(1)} %get-tuple-element.184) | copy-start | bytes 100
  681.4 68.1 %copy-start.41 = (f32[1,8]{1,0:T(1,128)}, f32[1,8]{1,0:T(1,128)S(1)}, u32[]{:S(2)}) copy-start(f32[1,8]{1,0:T(1,128)S(1)} %get-tuple-element.157) | copy-start | bytes 100
  681.5 68.0 %copy-start.47 = (f32[1,8]{1,0:T(1,128)}, f32[1,8]{1,0:T(1,128)S(1)}, u32[]{:S(2)}) copy-start(f32[1,8]{1,0:T(1,128)S(1)} %get-tuple-element.154) | copy-start | bytes 100
  681.5 68.0 %copy-start.49 = (f32[1,8]{1,0:T(1,128)}, f32[1,8]{1,0:T(1,128)S(1)}, u32[]{:S(2)}) copy-start(f32[1,8]{1,0:T(1,128)S(1)} %get-tuple-element.155) | copy-start | bytes 100
  681.5 68.0 %copy-start.51 = (f32[1,8]{1,0:T(1,128)}, f32[1,8]{1,0:T(1,128)S(1)}, u32[]{:S(2)}) copy-start(f32[1,8]{1,0:T(1,128)S(1)} %get-tuple-element.156) | copy-start | bytes 100
  712.8 36.7 %all-to-all-start.4 = ((bf16[8,3,192,8]{2,3,1,0:T(8,128)(2,1)}), bf16[8,3,192,8]{2,3,1,0:T(8,128)(2,1)S(1)}, u32[]{:S(2)}, u32[]{:S(2)}) async-start(bf16[8,3,192,8]{2,3,1,0:T(8,128)(2,1)} %broadcast_in_dim.56), calls=%async_computation.6 | async-start | bytes 196608 | tf_op jit(solution)/shard_map/all_to_all | solution.py:41
  716.2 83.2 %all-gather.21.cloned.1.call-start = ((), (), s32[]{:S(2)}) async-start(), calls=%async_computation.14 | async-start | bytes 1671168 | tf_op jit(solution)/shard_map/all_gather | solution.py:49
  717.2 55.5 %copy-start.14 = (f32[144,64]{1,0:T(8,128)}, f32[144,64]{1,0:T(8,128)S(1)}, u32[]{:S(2)}) copy-start(f32[144,64]{1,0:T(8,128)S(1)} %copy.427) | copy-start | bytes 110596
  745.6 27.0 %copy-start.17 = (f32[1,144,64]{2,1,0:T(8,128)}, f32[1,144,64]{2,1,0:T(8,128)S(1)}, u32[]{:S(2)}) copy-start(f32[1,144,64]{2,1,0:T(8,128)S(1)} %copy.470) | copy-start | bytes 110596
  777.6 16.4 %copy-start.20 = (f32[12,64]{1,0:T(8,128)}, f32[12,64]{1,0:T(8,128)S(1)}, u32[]{:S(2)}) copy-start(f32[12,64]{1,0:T(8,128)S(1)} %get-tuple-element.235) | copy-start | bytes 9220
  778.3 11.4 %all-to-all-start.5 = ((f32[8,1,768]{2,1,0:T(1,128)}), f32[8,1,768]{2,1,0:T(1,128)S(1)}, u32[]{:S(2)}, u32[]{:S(2)}) async-start(f32[8,1,768]{2,1,0:T(1,128)} %reshape.2146), calls=%async_computation.7 | async-start | bytes 49152 | tf_op jit(solution)/shard_map/all_to_all | solution.py:41
  783.5 57.7 %reduce-scatter.8.cloned.1.call-start = ((), (), s32[]{:S(2)}) async-start(), calls=%async_computation.11 | async-start | bytes 589824 | tf_op jit(solution)/shard_map/reduce_scatter | solution.py:58
  806.1 44.8 %copy-start.48 = (f32[1,8]{1,0:T(1,128)S(1)}, f32[1,8]{1,0:T(1,128)}, u32[]{:S(2)}) copy-start(f32[1,8]{1,0:T(1,128)} %copy-done.47) | copy-start | bytes 100
  806.1 44.8 %copy-start.50 = (f32[1,8]{1,0:T(1,128)S(1)}, f32[1,8]{1,0:T(1,128)}, u32[]{:S(2)}) copy-start(f32[1,8]{1,0:T(1,128)} %copy-done.49) | copy-start | bytes 100
  806.1 44.8 %copy-start.52 = (f32[1,8]{1,0:T(1,128)S(1)}, f32[1,8]{1,0:T(1,128)}, u32[]{:S(2)}) copy-start(f32[1,8]{1,0:T(1,128)} %copy-done.51) | copy-start | bytes 100
  (72 other events, 245.3 us)
Sparse Core Ops, SparseCore 0:
  51.3 47.5 all-gather.16
  467.7 32.7 reduce-scatter.3
  576.4 43.9 all-gather.18
  635.2 34.8 reduce-scatter.5
  747.4 44.0 all-gather.20
  806.2 34.8 reduce-scatter.7
where the time goes:
time: 863 us; the launch traced here: 859 us
  blocking collectives  543 us (63%)
  waiting for transfers between devices  111 us (13%)
  local copies, waits for them, and re-layouts  74.6 us (9%)
  matrix products  52.3 us (6%)
  other arithmetic  35.2 us (4%)
  starting transfers between devices  26.8 us (3%)
  between operations  16.3 us (2%)
    all_gather x4, blocking collectives, rows_first(): whole, at, outs = (lax.all_gather(both, axis, axis=0, tiled=True), 0, [])  397 us
    all_gather x6, blocking collectives, broadcast(): lax.all_gather(value, axis)  146 us
    reduce_scatter x3, waiting for transfers between devices, sent_together(): lax.psum_scatter(both, axis, scatter_dimension=dim, tiled=True)  103 us
    unnamed x246, local copies, waits for them, and re-layouts  31.3 us
    all_to_all x6, starting transfers between devices, copy_for_each(): return lax.all_to_all(copies, axis, split_axis=0, concat_axis=0, tiled=True)  25.9 us
  transfers between devices with their start and end apart: 12, of which 6 were waited for; matrix products, arithmetic and copies ran while one was open for 11% of the time, Pallas kernels for 0%

commit v1 on v0

v1 whole, which is shorter than its diff:
```python
import functools
import math

import jax
import jax.numpy as jnp
import numpy as np
from jax import lax
from jax.experimental import pallas as pl
from jax.experimental.pallas import tpu as pltpu
from jax.sharding import PartitionSpec as P

H = 12
C = 16
PQ = 4
PV = 8
BINS = 128
ITERS = 3
D = 384
HP = 16
ROWS = 64
COLS = 128
OWN = 8
NR = 16
NC = 8
SW = 512
RW = 768
QW = 640
FW = 1024
MIXW = 1792

NORM_EPSILON = 1e-05
MASKED_LOGIT = -100000.0
DEAD = -3e38
NORM_FLOOR = 0.1
THIRD = math.sqrt(1.0 / 3.0)
MESH = pl.DeviceIdType.MESH
F32 = jnp.float32
BF16 = jnp.bfloat16


def rotation_entries(b, c, d):
    inverse = 1.0 / (1.0 + b * b + c * c + d * d)
    entries = [
        1.0 + b * b - c * c - d * d,
        2.0 * (b * c - d),
        2.0 * (b * d + c),
        2.0 * (b * c + d),
        1.0 - b * b + c * c - d * d,
        2.0 * (c * d - b),
        2.0 * (b * d - c),
        2.0 * (c * d + b),
        1.0 - b * b - c * c + d * d,
    ]
    return [e * inverse for e in entries]


def layer_norm(values):
    center = values - jnp.mean(values, axis=-1, keepdims=True)
    spread = jnp.mean(center * center, axis=-1, keepdims=True)
    return center * lax.rsqrt(spread + NORM_EPSILON)


def column_maps():
    lane = np.arange(128)

    def scalars(at):
        f = np.arange(256)
        return np.where(f < H * C, at * H * C + f, -1)

    def points(base):
        comps = []
        for a in range(3):
            comps.append(np.where(lane < 96, base + a * H * PQ + lane % 48, -1))
        return np.concatenate(comps)

    values = np.concatenate(
        [np.where(lane < 96, 6 * H * PQ + a * H * PV + lane, -1) for a in range(3)]
    )
    scal = np.concatenate([scalars(0), scalars(1), scalars(2)])
    pts = np.concatenate([points(0), points(3 * H * PQ), values])
    return scal.reshape(1, -1).astype(np.int32), pts.reshape(1, -1).astype(np.int32)


def head_mask():
    f = np.arange(FW)
    lane = f % 128
    head = np.where(f < 256, f // C, np.where(lane < 96, (lane % 48) // PQ, lane - 96))
    ok = np.where(f < 256, f < H * C, lane < 96 + H)
    rows = np.arange(HP)[:, None]
    return ((rows == head[None]) & ok[None]).astype(np.float32)


def split2(x):
    hi = x.astype(BF16)
    return hi, (x - hi.astype(F32)).astype(BF16)


def mm(a, b):
    return jnp.dot(a, b, preferred_element_type=F32)


def dot3(x, w_hi, w_mid):
    hi, mid = split2(x)
    n = x.shape[0]
    both = mm(jnp.concatenate([hi, mid], axis=0), w_hi)
    return both[:n] + both[n:] + mm(hi, w_mid)


def lane_iota(rows):
    return lax.broadcasted_iota(jnp.int32, (rows, 128), 1)


def column(x, k):
    return jnp.broadcast_to(x[:, k : k + 1], (x.shape[0], 128))


def kernel(
    state0, pair_hbm, relpos, gain, wb_t, gamma, hmask, smap, pmap,
    wsc_hbm, wpt_hbm, wout_hbm, whid_hbm, wback_hbm, wframe,
    single_out, frames_out,
    pair_v, bias_v, wsc_f, wpt_f, wout_f, whid_f, wback_f,
    wp_hi, wp_mid, wmix_hi, wmix_mid, wloc_hi, wloc_mid, whid_hi, whid_mid, wback_hi, wback_mid,
    wfr_hi, wfr_mid,
    send_buf, row_recv, swap_recv, col_recv, sync_send, sync_recv, red_send, red_recv,
    qf, qmask, kf, vcat, idx_b, p_s, m_b, s_b, r_s, pair_s,
    copy_sem, row_ss, row_rs, swap_ss, swap_rs, col_ss, col_rs, sync_ss, sync_rs, red_ss, red_rs,
):
    r = lax.axis_index("row")
    c = lax.axis_index("col")
    swap_row = 2 * c + lax.rem(r, 2)
    swap_col = r // 2
    alone = swap_col == c
    slot = lax.rem(r, 2) * 8 + r // 2

    copies = [
        pltpu.make_async_copy(src, dst, copy_sem.at[k])
        for k, (src, dst) in enumerate(
            [
                (wsc_hbm, wsc_f),
                (wpt_hbm, wpt_f),
                (pair_hbm, pair_v),
                (wout_hbm, wout_f),
                (whid_hbm, whid_f),
                (wback_hbm, wback_f),
            ]
        )
    ]
    for cp in copies:
        cp.start()

    barrier = pltpu.get_barrier_semaphore()
    for d in range(1, NC):
        pl.semaphore_signal(
            barrier, inc=1, device_id=(r, lax.rem(c + d, NC)), device_id_type=MESH
        )
    for d in range(1, NR):
        pl.semaphore_signal(
            barrier, inc=1, device_id=(lax.rem(r + d, NR), c), device_id_type=MESH
        )

    @pl.when(jnp.logical_not(alone))
    def _():
        pl.semaphore_signal(barrier, inc=1, device_id=(swap_row, swap_col), device_id_type=MESH)
        pl.semaphore_wait(barrier, NC + NR - 1)

    @pl.when(alone)
    def _():
        pl.semaphore_wait(barrier, NC + NR - 2)

    send_buf[0] = state0[...]

    def row_copy(it, peer, at):
        return pltpu.make_async_remote_copy(
            src_ref=send_buf.at[it],
            dst_ref=row_recv.at[it, at],
            send_sem=row_ss.at[peer],
            recv_sem=row_rs.at[it, at],
            device_id=(r, peer),
            device_id_type=MESH,
        )

    def swap_copy(it):
        return pltpu.make_async_remote_copy(
            src_ref=send_buf.at[it],
            dst_ref=swap_recv.at[it],
            send_sem=swap_ss,
            recv_sem=swap_rs.at[it],
            device_id=(swap_row, swap_col),
            device_id_type=MESH,
        )

    def col_copy(it, peer, at):
        return pltpu.make_async_remote_copy(
            src_ref=swap_recv.at[it],
            dst_ref=col_recv.at[it, at],
            send_sem=col_ss.at[peer],
            recv_sem=col_rs.at[it, at],
            device_id=(peer, c),
            device_id_type=MESH,
        )

    def sync_copy(it, peer, at):
        return pltpu.make_async_remote_copy(
            src_ref=sync_send.at[it],
            dst_ref=sync_recv.at[it, at],
            send_sem=sync_ss.at[peer],
            recv_sem=sync_rs.at[it, at],
            device_id=(r, peer),
            device_id_type=MESH,
        )

    def red_copy(it, peer, at):
        return pltpu.make_async_remote_copy(
            src_ref=red_send.at[it, peer],
            dst_ref=red_recv.at[it, at],
            send_sem=red_ss.at[peer],
            recv_sem=red_rs.at[it, at],
            device_id=(r, peer),
            device_id_type=MESH,
        )

    def start_exchange(it):
        @pl.when(jnp.logical_not(alone))
        def _():
            swap_copy(it).start()

        for d in range(1, NC):
            row_copy(it, lax.rem(c + d, NC), c).start()
        row_recv[it, c] = send_buf[it]

    def prepare_weights():
        for cp in copies[:2]:
            cp.wait()
        for w_f, m_ref, widths, starts in (
            (wsc_f, smap, (256, 256, 256), (0, QW, 2 * QW)),
            (wpt_f, pmap, (384, 384, 384), (256, QW + 256, 2 * QW + 256)),
        ):
            hi, mid = split2(w_f[...])
            at = 0
            for width, start in zip(widths, starts):
                pick = (
                    lax.broadcasted_iota(jnp.int32, (w_f.shape[1], width), 0)
                    == m_ref[:, at : at + width]
                )
                pick = jnp.where(pick, 1.0, 0.0).astype(BF16)
                wp_hi[:, start : start + width] = mm(hi, pick).astype(BF16)
                wp_mid[:, start : start + width] = mm(mid, pick).astype(BF16)
                at += width
        for cp in copies[3:]:
            cp.wait()
        zeros64 = jnp.zeros((64, D), BF16)
        zeros32 = jnp.zeros((32, D), BF16)
        for part, (dst_mix, dst_loc) in enumerate(((wmix_hi, wloc_hi), (wmix_mid, wloc_mid))):
            dst_mix[0:192] = split2(wout_f[0:192])[part]
            dst_mix[192:256] = zeros64
            for k in range(4):
                dst_mix[256 + 384 * k : 640 + 384 * k] = split2(
                    wout_f[576 + 384 * k : 960 + 384 * k]
                )[part]
            for k in range(4):
                dst_loc[128 * k : 128 * k + 96] = split2(wout_f[192 + 96 * k : 288 + 96 * k])[part]
                dst_loc[128 * k + 96 : 128 * k + 128] = zeros32
        whid_hi[...], whid_mid[...] = split2(whid_f[...])
        wback_hi[...], wback_mid[...] = split2(wback_f[...])
        wfr_hi[...], wfr_mid[...] = split2(wframe[...])

    def to_global(f, y, width):
        comps = []
        x = [y[:, 128 * b : 128 * b + 128] for b in range(3)]
        keep = lane_iota(f.shape[0]) < width
        for a in range(3):
            g = (
                column(f, 3 * a) * x[0]
                + column(f, 3 * a + 1) * x[1]
                + column(f, 3 * a + 2) * x[2]
                + column(f, 9 + a)
            )
            comps.append(jnp.where(keep, g, 0.0))
        return comps

    def square_terms(comps):
        sq = comps[0] * comps[0] + comps[1] * comps[1] + comps[2] * comps[2]
        f = lax.broadcasted_iota(jnp.int32, (128, 128), 0)
        n = lax.broadcasted_iota(jnp.int32, (128, 128), 1)
        pick = jnp.where((f < 48) & (n == 96 + f // PQ), 1.0, 0.0).astype(BF16)
        hi, mid = split2(sq)
        lo = (sq - hi.astype(F32) - mid.astype(F32)).astype(BF16)
        total = (mm(hi, pick) + mm(mid, pick) + mm(lo, pick)) * gamma[...]
        hi, mid = split2(total)
        lo = (total - hi.astype(F32) - mid.astype(F32)).astype(BF16)
        return hi, mid, lo

    def query_features(it):
        s = row_recv[it].reshape(ROWS, SW)
        y = dot3(s[:, :D], wp_hi[:, :QW], wp_mid[:, :QW])
        qf[:, 0:256] = y[:, :256]
        comps = to_global(s[:, D:], y[:, 256:], 96)
        squares = square_terms(comps)
        lane = lane_iota(ROWS)
        for a in range(3):
            hi, mid = split2(comps[a] * gamma[...])
            ones = jnp.where(lane < 96 + H, 1.0, 0.0)
            qf[:, 256 + 128 * a : 384 + 128 * a] = jnp.where(lane < 96, hi.astype(F32), ones)
            qf[:, 640 + 128 * a : 768 + 128 * a] = jnp.where(
                lane < 48, mid.astype(F32), jnp.where(lane < 96, 0.0, squares[a].astype(F32))
            )

        mask = hmask[...]

        def spread(k, carry):
            for u in range(4):
                i = k * 4 + u
                row = jnp.broadcast_to(qf[pl.ds(i, 1), :], (HP, FW))
                at = pl.multiple_of(i * HP, HP)
                qmask[pl.ds(at, HP), :] = (row * mask).astype(BF16)
            return carry

        lax.fori_loop(0, ROWS // 4, spread, 0)

    def key_features(it):
        s = col_recv[it].reshape(COLS, SW)
        hi, mid = split2(s[:, :D])
        w_hi, w_mid = wp_hi[:, QW:], wp_mid[:, QW:]
        y = mm(hi, w_hi) + mm(mid, w_hi) + mm(hi, w_mid)
        kf[:, 0:256] = y[:, :256].astype(BF16)
        f = s[:, D:]
        comps = to_global(f, y[:, 256:QW], 96)
        squares = square_terms(comps)
        lane = lane_iota(COLS)
        zero = jnp.zeros((COLS, 128), F32)
        for a in range(3):
            hi, mid = split2(comps[a])
            hi, mid = hi.astype(F32), mid.astype(F32)
            sq = squares[a].astype(F32)
            kf[:, 256 + 128 * a : 384 + 128 * a] = jnp.where(
                lane < 48, hi, jnp.where(lane < 96, mid, sq)
            ).astype(BF16)
            ones = jnp.where((lane >= 96) & (lane < 96 + H), 1.0, zero)
            kf[:, 640 + 128 * a : 768 + 128 * a] = jnp.where(lane < 48, hi, ones).astype(BF16)
        v = y[:, QW : QW + 256].astype(BF16)
        vcat[0:COLS, 0:256] = v
        vcat[COLS : 2 * COLS, 0:256] = v
        vcat[2 * COLS :, 0:256] = jnp.zeros((COLS, 256), BF16)
        values = to_global(f, y[:, QW + 256 :], 96)
        for a in range(3):
            hi, mid = split2(values[a])
            at = 256 + 128 * a
            vcat[0:COLS, at : at + 128] = hi
            vcat[COLS : 2 * COLS, at : at + 128] = hi
            vcat[2 * COLS :, at : at + 128] = mid

    def prepare_pair():
        copies[2].wait()
        fq = row_recv[0].reshape(ROWS, SW)[:, D:]
        fk = col_recv[0].reshape(COLS, SW)[:, D:]
        idx_b[0:ROWS] = column(fq, 12)
        idx_b[ROWS:] = column(fq, 13)
        key_index = column(fk, 12)
        key_live = fk.T[13:14, :]
        lane = lax.broadcasted_iota(jnp.int32, (COLS, 128), 1).astype(F32)
        table = relpos[...]
        gains = gain[...]
        project = wb_t[...]

        def prepare(k, carry):
            for u in range(2):
                i = k * 2 + u
                offset = jnp.clip(key_index - idx_b[pl.ds(i, 1), :], -64.0, 63.0) + 64.0
                onehot = jnp.where(offset == lane, 1.0, 0.0).astype(BF16)
                x = pair_v[i].astype(F32) + mm(onehot, table)
                normed = (layer_norm(x) * gains).astype(BF16)
                pair_v[i] = normed
                bias = lax.dot_general(
                    project, normed, (((1,), (1,)), ((), ())), preferred_element_type=F32
                )
                live = key_live * idx_b[pl.ds(ROWS + i, 1), :] > 0.5
                at = pl.multiple_of(i * HP, HP)
                bias_v[pl.ds(at, HP), :] = jnp.where(live, bias * THIRD, DEAD)
            return carry

        lax.fori_loop(0, ROWS // 2, prepare, 0)

    def attend(it):
        keys = kf[...]
        rows = 128

        def logits_of(k, carry):
            at = pl.multiple_of(k * rows, rows)
            part = pl.ds(at, rows)
            acc = lax.dot_general(
                qmask[part, :], keys, (((1,), (1,)), ((), ())), preferred_element_type=F32
            )
            bias = bias_v[part, :]
            logits = jnp.where(bias > -1e38, acc * (THIRD / math.sqrt(C)) + bias, MASKED_LOGIT)
            top = jnp.max(logits, axis=-1, keepdims=True)
            p = jnp.exp(logits - top)
            m_b[part, :] = jnp.broadcast_to(top, (rows, 128))
            s_b[part, :] = jnp.broadcast_to(jnp.sum(p, axis=-1, keepdims=True), (rows, 128))
            hi, mid = split2(p)
            p_s[part, 0:128] = hi
            p_s[part, 128:256] = mid
            p_s[part, 256:384] = hi
            return carry

        lax.fori_loop(0, ROWS * HP // rows, logits_of, 0)

        lane = lane_iota(8)
        tops = jnp.zeros((8, 128), F32)
        sums = jnp.zeros((8, 128), F32)
        for g in range(8):
            for h in range(HP):
                src = pl.ds(8 * HP * g + h, 8, stride=HP)
                tops = jnp.where(lane == g * HP + h, m_b[src, :], tops)
                sums = jnp.where(lane == g * HP + h, s_b[src, :], sums)
        sync_send[it, 0:8] = tops
        sync_send[it, 8:16] = sums
        for d in range(1, NC):
            sync_copy(it, lax.rem(c + d, NC), c).start()
        sync_recv[it, c] = sync_send[it]

        def pair_sum(k, carry):
            for u in range(8):
                i = k * 8 + u
                at = pl.multiple_of(i * HP, HP)
                pair_s[pl.ds(at, HP), :] = mm(p_s[pl.ds(at, HP), 0:128], pair_v[i])
            return carry

        lax.fori_loop(0, ROWS // 8, pair_sum, 0)
        values = vcat[...]

        def value_sum(k, carry):
            at = pl.multiple_of(k * 256, 256)
            part = pl.ds(at, 256)
            y = mm(p_s[part, :], values)
            for t in range(5):
                r_s[t, part, :] = y[:, 128 * t : 128 * t + 128]
            return carry

        lax.fori_loop(0, ROWS * HP // 256, value_sum, 0)

        for d in range(1, NC):
            peer = lax.rem(c + d, NC)
            sync_copy(it, peer, peer).wait_recv()
        all_tops = [sync_recv[it, k, 0:8] for k in range(NC)]
        top = functools.reduce(jnp.maximum, all_tops)
        total = jnp.zeros((8, 128), F32)
        for k in range(NC):
            total = total + sync_recv[it, k, 8:16] * jnp.exp(all_tops[k] - top)
        factor = jnp.exp(tops - top) / total

        scale = []
        for h in range(H):
            scale.append(
                jnp.concatenate([column(factor, g * HP + h) for g in range(8)], axis=0)
            )

        wide = lane_iota(ROWS)
        tiles = []
        for t in range(5):
            out = jnp.zeros((ROWS, 128), F32)
            if t == 0:
                heads, first, size = range(0, 8), 0, C
            elif t == 1:
                heads, first, size = range(8, 12), 8, C
            else:
                heads, first, size = range(0, H), 0, PV
            for h in heads:
                part = r_s[t, pl.ds(h, ROWS, stride=HP), :] * scale[h]
                lo = (h - first) * size
                out = jnp.where((wide >= lo) & (wide < lo + size), part, out)
            tiles.append(out)
        pairs = [pair_s[pl.ds(h, ROWS, stride=HP), :] * scale[h] for h in range(H)]
        mixed_in = jnp.concatenate(tiles[:2] + pairs, axis=1)
        mixed = dot3(mixed_in, wmix_hi[...], wmix_mid[...])
        red_send[it, :, :, 0:D] = mixed.reshape(NC, OWN, D)
        for a in range(3):
            red_send[it, :, :, D + 128 * a : D + 128 * a + 128] = tiles[2 + a].reshape(NC, OWN, 128)
        for d in range(1, NC):
            red_copy(it, lax.rem(c + d, NC), c).start()
        red_recv[it, c] = red_send[it, c]

    def advance(it):
        for d in range(1, NC):
            peer = lax.rem(c + d, NC)
            red_copy(it, peer, peer).wait_recv()
        acc = red_recv[it, 0]
        for k in range(1, NC):
            acc = acc + red_recv[it, k]
        state = send_buf[it]
        frames = state[:, D:]
        single = state[:, :D]
        moved = [acc[:, D + 128 * a : D + 128 * a + 128] - column(frames, 9 + a) for a in range(3)]
        local = [
            column(frames, a) * moved[0]
            + column(frames, 3 + a) * moved[1]
            + column(frames, 6 + a) * moved[2]
            for a in range(3)
        ]
        lengths = jnp.sqrt(
            local[0] * local[0] + local[1] * local[1] + local[2] * local[2] + NORM_FLOOR
        )
        keep = lane_iota(OWN) < H * PV
        feats = jnp.concatenate([jnp.where(keep, x, 0.0) for x in local + [lengths]], axis=1)
        single = layer_norm(single + acc[:, :D] + dot3(feats, wloc_hi[...], wloc_mid[...]))
        hidden = jnp.maximum(dot3(single, whid_hi[...], whid_mid[...]), 0.0)
        single = layer_norm(single + dot3(hidden, wback_hi[...], wback_mid[...]))
        update = dot3(single, wfr_hi[...], wfr_mid[...])
        turn = rotation_entries(column(update, 0), column(update, 1), column(update, 2))
        rot = [column(frames, k) for k in range(9)]
        step = [column(update, 3 + k) for k in range(3)]
        new = [
            rot[3 * left] * turn[right]
            + rot[3 * left + 1] * turn[3 + right]
            + rot[3 * left + 2] * turn[6 + right]
            for left in range(3)
            for right in range(3)
        ] + [
            rot[3 * left] * step[0]
            + rot[3 * left + 1] * step[1]
            + rot[3 * left + 2] * step[2]
            + column(frames, 9 + left)
            for left in range(3)
        ]
        lane = lane_iota(OWN)
        out = frames
        for k, value in enumerate(new):
            out = jnp.where(lane == k, value, out)
        return single, out

    def iteration(it, carry):
        start_exchange(it)

        @pl.when(it == 0)
        def _():
            prepare_weights()

        @pl.when(alone)
        def _():
            swap_recv[it] = send_buf[it]

        @pl.when(jnp.logical_not(alone))
        def _():
            swap_copy(it).wait_recv()

        for d in range(1, NR):
            col_copy(it, lax.rem(r + d, NR), slot).start()
        col_recv[it, slot] = swap_recv[it]

        for d in range(1, NC):
            peer = lax.rem(c + d, NC)
            row_copy(it, peer, peer).wait_recv()
        query_features(it)
        for d in range(1, NR):
            peer = lax.rem(r + d, NR)
            col_copy(it, peer, lax.rem(peer, 2) * 8 + peer // 2).wait_recv()
        key_features(it)

        @pl.when(it == 0)
        def _():
            prepare_pair()

        attend(it)
        single, frames = advance(it)

        @pl.when(it < ITERS - 1)
        def _():
            send_buf[it + 1, :, 0:D] = single
            send_buf[it + 1, :, D:] = frames

        @pl.when(it == ITERS - 1)
        def _():
            single_out[...] = single
            frames_out[...] = frames

        @pl.when(jnp.logical_not(alone))
        def _():
            swap_copy(it).wait_send()

        for d in range(1, NC):
            peer = lax.rem(c + d, NC)
            row_copy(it, peer, c).wait_send()
            sync_copy(it, peer, c).wait_send()
            red_copy(it, peer, c).wait_send()
        for d in range(1, NR):
            col_copy(it, lax.rem(r + d, NR), slot).wait_send()
        return carry

    lax.fori_loop(0, ITERS, iteration, 0)


def body(
    pair, relpos, pair_gain, bias_weight, single, rotation_params, translation, residue_index,
    residue_mask, w_scalar, w_points, head_weights, w_out, w_hidden, w_back, w_frame,
):
    frames = jnp.stack(
        rotation_entries(rotation_params[0], rotation_params[1], rotation_params[2])
        + [translation[0], translation[1], translation[2]]
        + [residue_index.astype(F32), (residue_mask == 1).astype(F32)]
    )
    state0 = jnp.concatenate([single, frames.T, jnp.zeros((OWN, SW - D - 14), F32)], axis=1)
    scale = jax.nn.softplus(head_weights) * (math.sqrt(2.0 / (9.0 * PQ)) / 2.0)
    lane = np.arange(128)
    head = np.where(lane < 96, (lane % 48) // PQ, lane - 96)
    weight = np.where(lane < 96, 8.0, np.where(lane < 96 + H, -4.0, 0.0))
    expand = ((np.arange(H)[:, None] == head[None]) * weight[None]).astype(np.float32)
    gamma = jnp.sum(scale[:, None] * expand, axis=0, keepdims=True)
    wb_t = jnp.pad(bias_weight.T, ((0, HP - H), (0, 0)))
    wframe = jnp.pad(w_frame, ((0, 0), (0, 122)))
    smap, pmap = column_maps()

    vmem = pl.BlockSpec(memory_space=pltpu.VMEM)
    anyspace = pl.BlockSpec(memory_space=pl.ANY)
    V = pltpu.VMEM
    dma = pltpu.SemaphoreType.DMA
    scratch = [
        V((ROWS, COLS, 128), BF16),
        V((ROWS * HP, 128), F32),
        V((D, 576), F32),
        V((D, 576), F32),
        V((2112, D), F32),
        V((D, D), F32),
        V((D, D), F32),
        V((D, 3 * QW), BF16),
        V((D, 3 * QW), BF16),
        V((MIXW, D), BF16),
        V((MIXW, D), BF16),
        V((512, D), BF16),
        V((512, D), BF16),
        V((D, D), BF16),
        V((D, D), BF16),
        V((D, D), BF16),
        V((D, D), BF16),
        V((D, 128), BF16),
        V((D, 128), BF16),
        V((ITERS, OWN, SW), F32),
        V((ITERS, NC, OWN, SW), F32),
        V((ITERS, OWN, SW), F32),
        V((ITERS, NR, OWN, SW), F32),
        V((ITERS, 16, 128), F32),
        V((ITERS, NC, 16, 128), F32),
        V((ITERS, NC, OWN, RW), F32),
        V((ITERS, NC, OWN, RW), F32),
        V((ROWS, FW), F32),
        V((ROWS * HP, FW), BF16),
        V((COLS, FW), BF16),
        V((3 * COLS, QW), BF16),
        V((2 * ROWS, 128), F32),
        V((ROWS * HP, 384), BF16),
        V((ROWS * HP, 128), F32),
        V((ROWS * HP, 128), F32),
        V((5, ROWS * HP, 128), F32),
        V((ROWS * HP, 128), F32),
        dma((6,)),
        dma((NC,)),
        dma((ITERS, NC)),
        dma,
        dma((ITERS,)),
        dma((NR,)),
        dma((ITERS, NR)),
        dma((NC,)),
        dma((ITERS, NC)),
        dma((NC,)),
        dma((ITERS, NC)),
    ]
    state, tile = pl.pallas_call(
        kernel,
        out_shape=(
            jax.ShapeDtypeStruct((OWN, D), F32),
            jax.ShapeDtypeStruct((OWN, 128), F32),
        ),
        in_specs=[vmem, anyspace] + [vmem] * 7 + [anyspace] * 5 + [vmem],
        out_specs=(vmem, vmem),
        scratch_shapes=scratch,
        compiler_params=pltpu.CompilerParams(
            collective_id=0, has_side_effects=True, vmem_limit_bytes=60 * 1024 * 1024
        ),
        name="structure",
    )(
        state0, pair, relpos, pair_gain.reshape(1, 128), wb_t, gamma, head_mask(), smap, pmap,
        w_scalar, w_points, w_out, w_hidden, w_back, wframe,
    )
    return state, tile[:, :12].T


def solution(mesh):
    placed = (
        P("row", "col", None),
        P(),
        P(),
        P(),
        P(("row", "col"), None),
        P(None, ("row", "col")),
        P(None, ("row", "col")),
        P(("row", "col")),
        P(("row", "col")),
        P(),
        P(),
        P(),
        P(),
        P(),
        P(),
        P(),
    )
    return jax.shard_map(
        body,
        mesh=mesh,
        in_specs=placed,
        out_specs=(P(("row", "col"), None), P(None, ("row", "col"))),
        check_vma=False,
    )
```

time: 863 us -> 120 us (0.14)
  blocking collectives: 543 us -> 0 us
  waiting for transfers between devices: 111 us -> 0 us
  Pallas kernels: 0 us -> 103 us
  local copies, waits for them, and re-layouts: 74.6 us -> 11.3 us
  matrix products: 52.3 us -> 0 us
  other arithmetic: 35.2 us -> 4.68 us
  starting transfers between devices: 26.8 us -> 0 us
  between operations: 16.3 us -> 0.67 us
    all_gather x10 -> x0, blocking collectives: 543 us -> none  [the longest x4 397 us: rows_first(): whole, at, outs = (lax.all_gather(both, axis, axis=0, tiled=True), 0, [])]
    reduce_scatter x3 -> x0, waiting for transfers between devices: 103 us -> none  [sent_together(): lax.psum_scatter(both, axis, scatter_dimension=dim, tiled=True)]
    pallas_call x0 -> x1, Pallas kernels: none -> 103 us  [body(): pl.pallas_call(kernel, out_shape=(jax.ShapeDtypeStruct((OWN, D), F32), ja...]
    dot_general x35 -> x0, matrix products: 52.3 us -> none  [the longest x3 8.33 us: attend_block(): jnp.einsum('hij,ijc->hci', rounded, normed, preferred_element_type=jnp.fl...]
    all_to_all x6 -> x0, starting transfers between devices: 25.9 us -> none  [copy_for_each(): return lax.all_to_all(copies, axis, split_axis=0, concat_axis=0, tiled=True)]
    unnamed x246 -> x10, local copies, waits for them, and re-layouts: 31.3 us -> 6.93 us
    slice x22 -> x1, local copies, waits for them, and re-layouts: 11.5 us -> 0.8 us  [body(): rotation_params[0]]
  transfers between devices with their start and end apart: 12 -> 0, of which waited for: 6 -> 0; matrix products, arithmetic and copies ran while one was open for 11% -> 0% of each run, Pallas kernels for 0% -> 0%
where the time goes in v1:
time: 120 us; the launch traced here: 119 us
  Pallas kernels  103 us (86%)
  local copies, waits for them, and re-layouts  11.3 us (9%)
  other arithmetic  4.68 us (4%)
    pallas_call x1, Pallas kernels, body(): pl.pallas_call(kernel, out_shape=(jax.ShapeDtypeStruct((OWN, D), F32), ja...  103 us
    unnamed x10, local copies, waits for them, and re-layouts  6.93 us

profile of v1, /device:TPU:0, one launch (start us, length us, event | category | flops | bytes accessed | tf_op | source)
XLA Modules:
  0.0 119.3 jit_solution(12441838895420483596)
XLA Ops:
  0.6 0.0 copy-start
  0.6 0.7 convert_bitcast_fusion
  1.4 0.7 fusion
  2.0 0.7 fusion.1
  2.7 1.3 %multiply_reduce_fusion = f32[128]{0:T(128)} fusion(f32[12,128]{1,0:T(8,128)} %constant.25.clone, f32[12]{0:T(128)S(1)} %fusion.1), kind=kLoop, calls=%fused_computation.1 | loop fusion | flops 2944 | bytes 6704 | tf_op jit(solution)/shard_map/reduce_sum | solution.py:606
  4.0 0.1 pad.12.clone
  4.1 0.8 fusion.2
  4.9 0.1 copy.40
  5.0 0.1 copy.36
  5.0 0.1 copy.35
  5.1 0.1 copy.41
  5.2 0.1 copy.42
  5.3 1.3 %pad.8.wb_t = bf16[16,128]{1,0:T(8,128)(2,1)} pad(bf16[12,128]{1,0:T(8,128)(2,1)} %bitcast.11, bf16[]{:T(256)} %constant.9.clone.1), padding=0_4x0_0 | pad | bytes 7170 | tf_op jit(solution)/shard_map/jit(_pad)/pad | solution.py:607
  6.6 0.8 copy.34
  7.3 0.1 stack.25
  7.4 1.3 %maximum_maximum_fusion.state0 = f32[8,512]{1,0:T(8,128)} fusion(f32[8,14]{1,0:T(8,128)S(1)} %bitcast.10, f32[8,384]{1,0:T(8,128)} %param.24, f32[512]{0:T(512)S(1)} %pad.12.clone), kind=kLoop, calls=%fused_computation | loop fusion | flops 8192 | bytes 31168 | tf_op jit(solution)/shard_map/concatenate | solution.py:600
  8.7 0.8 copy.37
  9.6 0.7 pad.9.wframe
  10.3 2.5 %copy.38.wsc_hbm = f32[384,576]{1,0:T(8,128)} copy(f32[384,576]{0,1:T(8,128)} %param.29) | data formatting | bytes 1769472 | tf_op args[9]
  12.7 0.0 copy-done
  12.7 1.3 %copy.39.wpt_hbm = f32[384,576]{1,0:T(8,128)} copy(f32[384,576]{0,1:T(8,128)S(1)} %copy-done) | data formatting | bytes 1769472 | tf_op args[10]
  14.1 102.6 %structure.1 = (f32[8,384]{1,0:T(8,128)}, f32[8,128]{1,0:T(8,128)}) custom-call(f32[8,512]{1,0:T(8,128)} %maximum_maximum_fusion.state0, bf16[64,128,128]{2,1,0:T(8,128)(2,1)} %pair_hbm.1, bf16[128,128]{1,0:T(8,128)(2,1)} %relpos.1, f32[1,128]{1,0:T(1,128)} %bitcast.13, bf16[16,128]{1,0:T(8,128)(2,1)} %pad.8.wb_t, f32[1,128]{1,0:T(1,128)} %bitcast.12, ...), custom_call_target="tpu_custom_call" | custom-call | tf_op jit(solution)/shard_map/structure/pallas_call | solution.py:665
  116.7 1.3 %slice_bitcast_fusion = f32[12,8]{0,1:T(8,128)} fusion(f32[8,128]{1,0:T(8,128)} %get-tuple-element.5), kind=kLoop, calls=%fused_computation.2 | loop fusion | bytes 768 | tf_op jit(solution)/shard_map/transpose | solution.py:682
  118.0 1.3 %copy.44 = f32[8,384]{1,0:T(8,128)} copy(f32[8,384]{1,0:T(8,128)} %get-tuple-element.20) | data formatting | bytes 24576
  (2 shorter events, 0.0 us)
Async XLA Ops:
  0.6 12.1 %copy-start = (f32[384,576]{0,1:T(8,128)S(1)}, f32[384,576]{0,1:T(8,128)}, u32[]{:S(2)}) copy-start(f32[384,576]{0,1:T(8,128)} %param.30) | copy-start | bytes 2654212

commit v2 on v1

v2 whole, which is shorter than its diff:
```python
import functools
import math

import jax
import jax.numpy as jnp
from jax import lax
from jax.experimental import pallas as pl
from jax.experimental.pallas import tpu as pltpu
from jax.sharding import PartitionSpec as P

H = 12
C = 16
PQ = 4
PV = 8
BINS = 128
ITERS = 3
D = 384
HP = 16
ROWS = 64
COLS = 128
OWN = 8
NR = 16
NC = 8
SW = 512
RW = 768
QW = 640
FW = 1024
MIXW = 1792

NORM_EPSILON = 1e-05
MASKED_LOGIT = -100000.0
DEAD = -3e38
NORM_FLOOR = 0.1
THIRD = math.sqrt(1.0 / 3.0)
MESH = pl.DeviceIdType.MESH
F32 = jnp.float32
BF16 = jnp.bfloat16


def rotation_entries(b, c, d):
    inverse = 1.0 / (1.0 + b * b + c * c + d * d)
    entries = [
        1.0 + b * b - c * c - d * d,
        2.0 * (b * c - d),
        2.0 * (b * d + c),
        2.0 * (b * c + d),
        1.0 - b * b + c * c - d * d,
        2.0 * (c * d - b),
        2.0 * (b * d - c),
        2.0 * (c * d + b),
        1.0 - b * b - c * c + d * d,
    ]
    return [e * inverse for e in entries]


def layer_norm(values):
    center = values - jnp.mean(values, axis=-1, keepdims=True)
    spread = jnp.mean(center * center, axis=-1, keepdims=True)
    return center * lax.rsqrt(spread + NORM_EPSILON)


def split2(x):
    hi = x.astype(BF16)
    return hi, (x - hi.astype(F32)).astype(BF16)


def mm(a, b):
    return jnp.dot(a, b, preferred_element_type=F32)


def dot3(x, w_hi, w_mid):
    hi, mid = split2(x)
    n = x.shape[0]
    both = mm(jnp.concatenate([hi, mid], axis=0), w_hi)
    return both[:n] + both[n:] + mm(hi, w_mid)


def lane_iota(rows):
    return lax.broadcasted_iota(jnp.int32, (rows, 128), 1)


def pad_lanes(x):
    return jnp.concatenate([x, jnp.zeros((x.shape[0], 128 - x.shape[1]), x.dtype)], axis=1)


def column(x, k):
    return jnp.broadcast_to(x[:, k : k + 1], (x.shape[0], 128))


def kernel(
    single_in, rotation_in, translation_in, index_in, live_in, head_in, relpos, gain, wb_in, wframe,
    pair_hbm, wsc_hbm, wpt_hbm, wout_hbm, whid_hbm, wback_hbm,
    single_out, frames_out,
    pair_v, bias_v, wsc_f, wpt_f, wout_f, whid_f, wback_f, wfr_f,
    wp_hi, wp_mid, wmix_hi, wmix_mid, wloc_hi, wloc_mid, whid_hi, whid_mid, wback_hi, wback_mid,
    wfr_hi, wfr_mid, wb_s, small, gamma, hmask, centre,
    send_buf, row_recv, swap_recv, col_recv, sync_send, sync_recv, mix_send, mix_recv,
    pts_send, pts_recv,
    qf, qmask, kf, vcat, idx_b, p_s, m_b, s_b, r_s, pair_s,
    copy_sem, row_ss, row_rs, swap_ss, swap_rs, col_ss, col_rs, sync_ss, sync_rs,
    mix_ss, mix_rs, pts_ss, pts_rs,
):
    r = lax.axis_index("row")
    c = lax.axis_index("col")
    core = lax.rem(r, 2)
    z = lax.rem(r // 2, 4)
    y_hi = r // 8
    x = lax.rem(c, 4)
    y_lo = c // 4
    to_row = y_lo * 8 + lax.rem(2 * z + 6 - x, 4) * 2 + core
    to_col = y_hi * 4 + z
    from_row = y_lo * 8 + x * 2 + core
    from_col = y_hi * 4 + lax.rem(2 * x + 6 - z, 4)

    def slot_of(row):
        return lax.rem(row, 2) * 8 + (row // 8) * 4 + lax.rem(2 * x + 6 - lax.rem(row // 2, 4), 4)

    slot = slot_of(r)

    copies = [
        pltpu.make_async_copy(src, dst, copy_sem.at[k])
        for k, (src, dst) in enumerate(
            [
                (wsc_hbm, wsc_f),
                (wpt_hbm, wpt_f),
                (pair_hbm, pair_v),
                (wout_hbm, wout_f),
                (whid_hbm, whid_f),
                (wback_hbm, wback_f),
            ]
        )
    ]
    for cp in copies:
        cp.start()

    barrier = pltpu.get_barrier_semaphore()
    for d in range(1, NC):
        pl.semaphore_signal(
            barrier, inc=1, device_id=(r, lax.rem(c + d, NC)), device_id_type=MESH
        )
    for d in range(1, NR):
        pl.semaphore_signal(
            barrier, inc=1, device_id=(lax.rem(r + d, NR), c), device_id_type=MESH
        )
    pl.semaphore_signal(barrier, inc=1, device_id=(from_row, from_col), device_id_type=MESH)

    small[...] = jnp.zeros_like(small)
    entries = rotation_entries(rotation_in[0:1], rotation_in[1:2], rotation_in[2:3])
    for k, row in enumerate(
        entries
        + [translation_in[k : k + 1] for k in range(3)]
        + [index_in[...].astype(F32), jnp.where(live_in[...] == 1, 1.0, 0.0)]
    ):
        small[k : k + 1, 0:OWN] = row
    head = head_in[...]
    positive = jnp.maximum(head, 0.0) + jnp.log1p(jnp.exp(-jnp.abs(head)))
    small[14:15, 0:H] = positive * (math.sqrt(2.0 / (9.0 * PQ)) / 2.0)
    turned = small[...].T
    send_buf[0, :, 0:D] = single_in[...]
    send_buf[0, :, D:] = jnp.where(lane_iota(OWN) < 14, pad_lanes(turned[0:OWN]), 0.0)

    lane = lane_iota(HP)
    head_row = lax.broadcasted_iota(jnp.int32, (HP, 128), 0)
    low = lane < 96
    owner = jnp.where(low, lax.rem(lane, 48) // PQ, lane - 96)
    own = (owner == head_row) & (lane < 96 + H)
    spread_scale = jnp.where(own, jnp.where(low, 8.0, -4.0), 0.0)
    gamma[...] = jnp.sum(
        jnp.broadcast_to(turned[0:HP, 14:15], (HP, 128)) * spread_scale, axis=0, keepdims=True
    )
    for t in range(2):
        own_scalar = (lane + 128 * t) // C == head_row
        hmask[:, 128 * t : 128 * t + 128] = jnp.where(own_scalar & (head_row < H), 1.0, 0.0)
    for t in range(2, 8):
        hmask[:, 128 * t : 128 * t + 128] = jnp.where(own & (head_row < H), 1.0, 0.0)

    with jax.named_scope("barrier"):
        pl.semaphore_wait(barrier, NC + NR - 1)

    def row_copy(it, peer, at):
        return pltpu.make_async_remote_copy(
            src_ref=send_buf.at[it],
            dst_ref=row_recv.at[it, at],
            send_sem=row_ss.at[peer],
            recv_sem=row_rs.at[it, at],
            device_id=(r, peer),
            device_id_type=MESH,
        )

    def swap_copy(it):
        return pltpu.make_async_remote_copy(
            src_ref=send_buf.at[it],
            dst_ref=swap_recv.at[it],
            send_sem=swap_ss,
            recv_sem=swap_rs.at[it],
            device_id=(to_row, to_col),
            device_id_type=MESH,
        )

    def col_copy(it, peer, at):
        return pltpu.make_async_remote_copy(
            src_ref=swap_recv.at[it],
            dst_ref=col_recv.at[it, at],
            send_sem=col_ss.at[peer],
            recv_sem=col_rs.at[it, at],
            device_id=(peer, c),
            device_id_type=MESH,
        )

    def sync_copy(it, peer, at):
        return pltpu.make_async_remote_copy(
            src_ref=sync_send.at[it],
            dst_ref=sync_recv.at[it, at],
            send_sem=sync_ss.at[peer],
            recv_sem=sync_rs.at[it, at],
            device_id=(r, peer),
            device_id_type=MESH,
        )

    def mix_copy(it, peer, at):
        return pltpu.make_async_remote_copy(
            src_ref=mix_send.at[it, peer],
            dst_ref=mix_recv.at[it, at],
            send_sem=mix_ss.at[peer],
            recv_sem=mix_rs.at[it, at],
            device_id=(r, peer),
            device_id_type=MESH,
        )

    def pts_copy(it, peer, at):
        return pltpu.make_async_remote_copy(
            src_ref=pts_send.at[it, peer],
            dst_ref=pts_recv.at[it, at],
            send_sem=pts_ss.at[peer],
            recv_sem=pts_rs.at[it, at],
            device_id=(r, peer),
            device_id_type=MESH,
        )

    def start_exchange(it):
        swap_copy(it).start()
        for d in range(1, NC):
            row_copy(it, lax.rem(c + d, NC), c).start()
        row_recv[it, c] = send_buf[it]

    def prepare_projection():
        for cp in copies[:2]:
            cp.wait()
        zeros64 = jnp.zeros((64, D), F32)
        zeros32 = jnp.zeros((32, D), F32)

        def place(block, rows):
            hi, mid = split2(rows.T)
            wp_hi[:, 128 * block : 128 * block + 128] = hi
            wp_mid[:, 128 * block : 128 * block + 128] = mid

        for g in range(3):
            at = g * H * C
            place(5 * g, wsc_f[at : at + 128])
            place(5 * g + 1, jnp.concatenate([wsc_f[at + 128 : at + 192], zeros64], axis=0))
            for a in range(3):
                if g < 2:
                    first = g * 144 + 48 * a
                    part = wpt_f[first : first + 48]
                    rows = jnp.concatenate([part, part, zeros32], axis=0)
                else:
                    rows = jnp.concatenate(
                        [wpt_f[288 + 96 * a : 384 + 96 * a], zeros32], axis=0
                    )
                place(5 * g + 2 + a, rows)

    def prepare_weights():
        for cp in copies[3:]:
            cp.wait()
        zeros64 = jnp.zeros((64, D), BF16)
        zeros32 = jnp.zeros((32, D), BF16)
        for part, (dst_mix, dst_loc) in enumerate(((wmix_hi, wloc_hi), (wmix_mid, wloc_mid))):
            dst_mix[0:192] = split2(wout_f[0:192])[part]
            dst_mix[192:256] = zeros64
            for k in range(4):
                dst_mix[256 + 384 * k : 640 + 384 * k] = split2(
                    wout_f[576 + 384 * k : 960 + 384 * k]
                )[part]
            for k in range(4):
                dst_loc[128 * k : 128 * k + 96] = split2(wout_f[192 + 96 * k : 288 + 96 * k])[part]
                dst_loc[128 * k + 96 : 128 * k + 128] = zeros32
        whid_hi[...], whid_mid[...] = split2(whid_f[...])
        wback_hi[...], wback_mid[...] = split2(wback_f[...])
        wfr_f[...] = jnp.zeros_like(wfr_f)
        wfr_f[0:6] = wframe[...]
        wfr_hi[...], wfr_mid[...] = split2(wfr_f[...].T)

    def to_global(f, y, width):
        comps = []
        x = [y[:, 128 * b : 128 * b + 128] for b in range(3)]
        keep = lane_iota(f.shape[0]) < width
        for a in range(3):
            g = (
                column(f, 3 * a) * x[0]
                + column(f, 3 * a + 1) * x[1]
                + column(f, 3 * a + 2) * x[2]
                + column(f, 9 + a)
            )
            comps.append(jnp.where(keep, g, 0.0))
        return comps

    def square_terms(comps):
        sq = comps[0] * comps[0] + comps[1] * comps[1] + comps[2] * comps[2]
        f = lax.broadcasted_iota(jnp.int32, (128, 128), 0)
        n = lax.broadcasted_iota(jnp.int32, (128, 128), 1)
        pick = jnp.where((f < 48) & (n == 96 + f // PQ), 1.0, 0.0).astype(BF16)
        hi, mid = split2(sq)
        lo = (sq - hi.astype(F32) - mid.astype(F32)).astype(BF16)
        total = (mm(hi, pick) + mm(mid, pick) + mm(lo, pick)) * gamma[...]
        hi, mid = split2(total)
        lo = (total - hi.astype(F32) - mid.astype(F32)).astype(BF16)
        return hi, mid, lo

    def query_features(it):
        s = row_recv[it].reshape(ROWS, SW)
        y = dot3(s[:, :D], wp_hi[:, :QW], wp_mid[:, :QW])
        qf[:, 0:256] = y[:, :256]
        comps = to_global(s[:, D:], y[:, 256:], 96)
        squares = square_terms(comps)
        lane = lane_iota(ROWS)
        for a in range(3):
            hi, mid = split2(comps[a] * gamma[...])
            ones = jnp.where(lane < 96 + H, 1.0, 0.0)
            qf[:, 256 + 128 * a : 384 + 128 * a] = jnp.where(lane < 96, hi.astype(F32), ones)
            qf[:, 640 + 128 * a : 768 + 128 * a] = jnp.where(
                lane < 48, mid.astype(F32), jnp.where(lane < 96, 0.0, squares[a].astype(F32))
            )

        mask = hmask[...]

        def spread(k, carry):
            for u in range(4):
                i = k * 4 + u
                row = jnp.broadcast_to(qf[pl.ds(i, 1), :], (HP, FW))
                at = pl.multiple_of(i * HP, HP)
                qmask[pl.ds(at, HP), :] = (row * mask).astype(BF16)
            return carry

        lax.fori_loop(0, ROWS // 4, spread, 0)

    def key_features(it):
        s = col_recv[it].reshape(COLS, SW)
        hi, mid = split2(s[:, :D])
        w_hi, w_mid = wp_hi[:, QW:], wp_mid[:, QW:]
        y = mm(hi, w_hi) + mm(mid, w_hi) + mm(hi, w_mid)
        kf[:, 0:256] = y[:, :256].astype(BF16)
        f = s[:, D:]
        comps = to_global(f, y[:, 256:QW], 96)
        squares = square_terms(comps)
        lane = lane_iota(COLS)
        zero = jnp.zeros((COLS, 128), F32)
        for a in range(3):
            hi, mid = split2(comps[a])
            hi, mid = hi.astype(F32), mid.astype(F32)
            sq = squares[a].astype(F32)
            kf[:, 256 + 128 * a : 384 + 128 * a] = jnp.where(
                lane < 48, hi, jnp.where(lane < 96, mid, sq)
            ).astype(BF16)
            ones = jnp.where((lane >= 96) & (lane < 96 + H), 1.0, zero)
            kf[:, 640 + 128 * a : 768 + 128 * a] = jnp.where(lane < 48, hi, ones).astype(BF16)
        vcat[0:COLS, 0:256] = y[:, QW : QW + 256].astype(BF16)
        vcat[COLS:, 0:256] = jnp.zeros((COLS, 256), BF16)
        values = to_global(f, y[:, QW + 256 :], 96)
        for a in range(3):
            hi, mid = split2(values[a])
            at = 256 + 128 * a
            vcat[0:COLS, at : at + 128] = hi
            vcat[COLS:, at : at + 128] = mid

    def prepare_pair():
        copies[2].wait()
        fq = row_recv[0].reshape(ROWS, SW)[:, D:]
        fk = col_recv[0].reshape(COLS, SW)[:, D:]
        idx_b[0:ROWS] = column(fq, 12)
        idx_b[ROWS:] = column(fq, 13)
        key_index = column(fk, 12)
        key_live = fk.T[13:14, :]
        shape = (COLS, 128)
        lane = lax.broadcasted_iota(jnp.int32, shape, 1).astype(F32) - 64.0
        same = lax.broadcasted_iota(jnp.int32, shape, 0) == lax.broadcasted_iota(jnp.int32, shape, 1)
        table = relpos[...].astype(F32)
        hi, mid = split2(table - jnp.mean(table, axis=-1, keepdims=True))
        centre[0:128] = jnp.where(same, 1.0 - 1.0 / 128.0, -1.0 / 128.0).astype(BF16)
        centre[128:256] = hi
        centre[256:384] = mid
        wb_s[...] = jnp.zeros_like(wb_s)
        wb_s[0:H] = wb_in[...].astype(F32)
        project = wb_s[...].astype(BF16)
        gains = gain[...]
        step = 8

        def prepare(k, carry):
            first = k * step
            centres = []
            for u in range(step):
                offset = jnp.clip(key_index - idx_b[pl.ds(first + u, 1), :], -64.0, 63.0)
                onehot = jnp.where(offset == lane, 1.0, 0.0).astype(BF16)
                both = jnp.concatenate([pair_v[first + u], onehot, onehot], axis=1)
                centres.append(mm(both, centre[...]))
            for u in range(step):
                spread = jnp.mean(centres[u] * centres[u], axis=-1, keepdims=True)
                normed = (centres[u] * lax.rsqrt(spread + NORM_EPSILON) * gains).astype(BF16)
                pair_v[first + u] = normed
                bias = lax.dot_general(
                    project, normed, (((1,), (1,)), ((), ())), preferred_element_type=F32
                )
                live = key_live * idx_b[pl.ds(ROWS + first + u, 1), :] > 0.5
                at = pl.multiple_of((first + u) * HP, HP)
                bias_v[pl.ds(at, HP), :] = jnp.where(live, bias * THIRD, DEAD)
            return carry

        lax.fori_loop(0, ROWS // step, prepare, 0)

    def attend(it):
        keys = kf[...]
        rows = 256
        for k in range(ROWS * HP // rows):
            part = pl.ds(k * rows, rows)
            acc = lax.dot_general(
                qmask[part, :], keys, (((1,), (1,)), ((), ())), preferred_element_type=F32
            )
            bias = bias_v[part, :]
            logits = jnp.where(bias > -1e38, acc * (THIRD / math.sqrt(C)) + bias, MASKED_LOGIT)
            top = jnp.max(logits, axis=-1, keepdims=True)
            p = jnp.exp(logits - top).astype(BF16)
            m_b[part, :] = jnp.broadcast_to(top, (rows, 128))
            total = jnp.sum(p.astype(F32), axis=-1, keepdims=True)
            s_b[part, :] = jnp.broadcast_to(total, (rows, 128))
            p_s[part, 0:128] = p
            p_s[part, 128:256] = p

        lane = lane_iota(8)
        tops = jnp.zeros((8, 128), F32)
        sums = jnp.zeros((8, 128), F32)
        for g in range(8):
            for h in range(HP):
                src = pl.ds(8 * HP * g + h, 8, stride=HP)
                tops = jnp.where(lane == g * HP + h, m_b[src, :], tops)
                sums = jnp.where(lane == g * HP + h, s_b[src, :], sums)
        sync_send[it, 0:8] = tops
        sync_send[it, 8:16] = sums
        for d in range(1, NC):
            sync_copy(it, lax.rem(c + d, NC), c).start()
        sync_recv[it, c] = sync_send[it]

        for i in range(ROWS):
            part = pl.ds(i * HP, HP)
            pair_s[part, :] = mm(p_s[part, 0:128], pair_v[i])
        values = vcat[...]
        for k in range(4):
            part = pl.ds(k * 256, 256)
            y = mm(p_s[part, :], values)
            for t in range(5):
                r_s[t, part, :] = y[:, 128 * t : 128 * t + 128]

        with jax.named_scope("wait_sync"):
            for d in range(1, NC):
                peer = lax.rem(c + d, NC)
                sync_copy(it, peer, peer).wait_recv()
        all_tops = [sync_recv[it, k, 0:8] for k in range(NC)]
        top = functools.reduce(jnp.maximum, all_tops)
        total = jnp.zeros((8, 128), F32)
        for k in range(NC):
            total = total + sync_recv[it, k, 8:16] * jnp.exp(all_tops[k] - top)
        factor = jnp.exp(tops - top) / total

        scale = []
        for h in range(H):
            scale.append(
                jnp.concatenate([column(factor, g * HP + h) for g in range(8)], axis=0)
            )

        wide = lane_iota(ROWS)
        tiles = {}
        for t in (2, 3, 4, 0, 1):
            out = jnp.zeros((ROWS, 128), F32)
            if t == 0:
                heads, first, size = range(0, 8), 0, C
            elif t == 1:
                heads, first, size = range(8, 12), 8, C
            else:
                heads, first, size = range(0, H), 0, PV
            for h in heads:
                part = r_s[t, pl.ds(h, ROWS, stride=HP), :] * scale[h]
                lo = (h - first) * size
                out = jnp.where((wide >= lo) & (wide < lo + size), part, out)
            tiles[t] = out
        for a in range(3):
            pts_send[it, :, :, 128 * a : 128 * a + 128] = tiles[2 + a].reshape(NC, OWN, 128)
        for d in range(1, NC):
            pts_copy(it, lax.rem(c + d, NC), c).start()
        pairs = [pair_s[pl.ds(h, ROWS, stride=HP), :] * scale[h] for h in range(H)]
        mixed_in = jnp.concatenate([tiles[0], tiles[1]] + pairs, axis=1)
        mixed = dot3(mixed_in, wmix_hi[...], wmix_mid[...])
        mix_send[it] = mixed.reshape(NC, OWN, D)
        for d in range(1, NC):
            mix_copy(it, lax.rem(c + d, NC), c).start()
        pts_recv[it, c] = pts_send[it, c]
        mix_recv[it, c] = mix_send[it, c]

    def advance(it):
        with jax.named_scope("wait_pts"):
            for d in range(1, NC):
                peer = lax.rem(c + d, NC)
                pts_copy(it, peer, peer).wait_recv()
        points = pts_recv[it, 0]
        for k in range(1, NC):
            points = points + pts_recv[it, k]
        state = send_buf[it]
        frames = state[:, D:]
        single = state[:, :D]
        moved = [points[:, 128 * a : 128 * a + 128] - column(frames, 9 + a) for a in range(3)]
        local = [
            column(frames, a) * moved[0]
            + column(frames, 3 + a) * moved[1]
            + column(frames, 6 + a) * moved[2]
            for a in range(3)
        ]
        lengths = jnp.sqrt(
            local[0] * local[0] + local[1] * local[1] + local[2] * local[2] + NORM_FLOOR
        )
        keep = lane_iota(OWN) < H * PV
        feats = jnp.concatenate([jnp.where(keep, x, 0.0) for x in local + [lengths]], axis=1)
        single = single + dot3(feats, wloc_hi[...], wloc_mid[...])
        with jax.named_scope("wait_mix"):
            for d in range(1, NC):
                peer = lax.rem(c + d, NC)
                mix_copy(it, peer, peer).wait_recv()
        for k in range(NC):
            single = single + mix_recv[it, k]
        single = layer_norm(single)
        hidden = jnp.maximum(dot3(single, whid_hi[...], whid_mid[...]), 0.0)
        single = layer_norm(single + dot3(hidden, wback_hi[...], wback_mid[...]))
        update = dot3(single, wfr_hi[...], wfr_mid[...])
        turn = rotation_entries(column(update, 0), column(update, 1), column(update, 2))
        rot = [column(frames, k) for k in range(9)]
        step = [column(update, 3 + k) for k in range(3)]
        new = [
            rot[3 * left] * turn[right]
            + rot[3 * left + 1] * turn[3 + right]
            + rot[3 * left + 2] * turn[6 + right]
            for left in range(3)
            for right in range(3)
        ] + [
            rot[3 * left] * step[0]
            + rot[3 * left + 1] * step[1]
            + rot[3 * left + 2] * step[2]
            + column(frames, 9 + left)
            for left in range(3)
        ]
        lane = lane_iota(OWN)
        out = frames
        for k, value in enumerate(new):
            out = jnp.where(lane == k, value, out)
        return single, out

    def iteration(it, carry):
        with jax.named_scope("start"):
            start_exchange(it)

            @pl.when(it == 0)
            def _():
                prepare_projection()

        with jax.named_scope("wait_swap"):
            swap_copy(it).wait_recv()
        with jax.named_scope("send_col"):
            for d in range(1, NR):
                col_copy(it, lax.rem(r + d, NR), slot).start()
            col_recv[it, slot] = swap_recv[it]

            @pl.when(it == 0)
            def _():
                prepare_weights()

        with jax.named_scope("wait_row"):
            for d in range(1, NC):
                peer = lax.rem(c + d, NC)
                row_copy(it, peer, peer).wait_recv()
        with jax.named_scope("query"):
            query_features(it)
        with jax.named_scope("wait_col"):
            for d in range(1, NR):
                peer = lax.rem(r + d, NR)
                col_copy(it, peer, slot_of(peer)).wait_recv()
        with jax.named_scope("key"):
            key_features(it)
        with jax.named_scope("prep_pair"):

            @pl.when(it == 0)
            def _():
                prepare_pair()

        with jax.named_scope("attend"):
            attend(it)
        with jax.named_scope("advance"):
            single, frames = advance(it)

            @pl.when(it < ITERS - 1)
            def _():
                send_buf[it + 1, :, 0:D] = single
                send_buf[it + 1, :, D:] = frames

            @pl.when(it == ITERS - 1)
            def _():
                single_out[...] = single
                frames_out[...] = frames[:, 0:12]

        with jax.named_scope("wait_send"):
            swap_copy(it).wait_send()
            for d in range(1, NC):
                peer = lax.rem(c + d, NC)
                row_copy(it, peer, c).wait_send()
                sync_copy(it, peer, c).wait_send()
                pts_copy(it, peer, c).wait_send()
                mix_copy(it, peer, c).wait_send()
            for d in range(1, NR):
                col_copy(it, lax.rem(r + d, NR), slot).wait_send()
        return carry

    lax.fori_loop(0, ITERS, iteration, 0)


def body(
    pair, relpos, pair_gain, bias_weight, single, rotation_params, translation, residue_index,
    residue_mask, w_scalar, w_points, head_weights, w_out, w_hidden, w_back, w_frame,
):
    vmem = pl.BlockSpec(memory_space=pltpu.VMEM)
    anyspace = pl.BlockSpec(memory_space=pl.ANY)
    V = pltpu.VMEM
    dma = pltpu.SemaphoreType.DMA
    scratch = [
        V((ROWS, COLS, 128), BF16),
        V((ROWS * HP, 128), F32),
        V((576, D), F32),
        V((576, D), F32),
        V((2112, D), F32),
        V((D, D), F32),
        V((D, D), F32),
        V((128, D), F32),
        V((D, 3 * QW), BF16),
        V((D, 3 * QW), BF16),
        V((MIXW, D), BF16),
        V((MIXW, D), BF16),
        V((512, D), BF16),
        V((512, D), BF16),
        V((D, D), BF16),
        V((D, D), BF16),
        V((D, D), BF16),
        V((D, D), BF16),
        V((D, 128), BF16),
        V((D, 128), BF16),
        V((HP, 128), F32),
        V((HP, 128), F32),
        V((1, 128), F32),
        V((HP, FW), F32),
        V((3 * 128, 128), BF16),
        V((ITERS, OWN, SW), F32),
        V((ITERS, NC, OWN, SW), F32),
        V((ITERS, OWN, SW), F32),
        V((ITERS, NR, OWN, SW), F32),
        V((ITERS, 16, 128), F32),
        V((ITERS, NC, 16, 128), F32),
        V((ITERS, NC, OWN, D), F32),
        V((ITERS, NC, OWN, D), F32),
        V((ITERS, NC, OWN, D), F32),
        V((ITERS, NC, OWN, D), F32),
        V((ROWS, FW), F32),
        V((ROWS * HP, FW), BF16),
        V((COLS, FW), BF16),
        V((2 * COLS, QW), BF16),
        V((2 * ROWS, 128), F32),
        V((ROWS * HP, 256), BF16),
        V((ROWS * HP, 128), F32),
        V((ROWS * HP, 128), F32),
        V((5, ROWS * HP, 128), F32),
        V((ROWS * HP, 128), F32),
        dma((6,)),
        dma((NC,)),
        dma((ITERS, NC)),
        dma,
        dma((ITERS,)),
        dma((NR,)),
        dma((ITERS, NR)),
        dma((NC,)),
        dma((ITERS, NC)),
        dma((NC,)),
        dma((ITERS, NC)),
        dma((NC,)),
        dma((ITERS, NC)),
    ]
    state, frames = pl.pallas_call(
        kernel,
        out_shape=(
            jax.ShapeDtypeStruct((OWN, D), F32),
            jax.ShapeDtypeStruct((OWN, 12), F32),
        ),
        in_specs=[vmem] * 10 + [anyspace] * 6,
        out_specs=(vmem, vmem),
        scratch_shapes=scratch,
        compiler_params=pltpu.CompilerParams(
            collective_id=0, has_side_effects=True, vmem_limit_bytes=60 * 1024 * 1024
        ),
        name="structure",
    )(
        single, rotation_params, translation, residue_index.reshape(1, OWN),
        residue_mask.reshape(1, OWN), head_weights.reshape(1, H), relpos,
        pair_gain.reshape(1, 128), bias_weight.T, w_frame.T,
        pair, w_scalar.T, w_points.T, w_out, w_hidden, w_back,
    )
    return state, frames.T


def solution(mesh):
    placed = (
        P("row", "col", None),
        P(),
        P(),
        P(),
        P(("row", "col"), None),
        P(None, ("row", "col")),
        P(None, ("row", "col")),
        P(("row", "col")),
        P(("row", "col")),
        P(),
        P(),
        P(),
        P(),
        P(),
        P(),
        P(),
    )
    return jax.shard_map(
        body,
        mesh=mesh,
        in_specs=placed,
        out_specs=(P(("row", "col"), None), P(None, ("row", "col"))),
        check_vma=False,
    )
```

time: 120 us -> 85.9 us (0.72)
  Pallas kernels: 103 us -> 82.4 us
  local copies, waits for them, and re-layouts: 11.3 us -> 2.57 us
  other arithmetic: 4.68 us -> 0 us
    pallas_call x1, Pallas kernels: 103 us -> 82.4 us  [body(): pl.pallas_call(kernel, out_shape=(jax.ShapeDtypeStruct((OWN, D), F32), ja...]
    unnamed x10 -> x2, local copies, waits for them, and re-layouts: 6.93 us -> 2.57 us
    pad x2 -> x0, local copies, waits for them, and re-layouts: 1.98 us -> none  [the longest x1 1.28 us: body(): wb_t = jnp.pad(bias_weight.T, ((0, HP - H), (0, 0)))]
    another operation x2 -> x0, other arithmetic: 1.39 us -> none  [body(): jnp.stack(rotation_entries(rotation_params[0], rotation_params[1], rotati...]
    concatenate x1 -> x0, other arithmetic: 1.31 us -> none  [body(): jnp.concatenate([single, frames.T, jnp.zeros((OWN, SW - D - 14), F32)], a...]
    reduce_sum x1 -> x0, other arithmetic: 1.3 us -> none  [body(): gamma = jnp.sum(scale[:, None] * expand, axis=0, keepdims=True)]
    transpose x1 -> x0, local copies, waits for them, and re-layouts: 1.28 us -> none  [body(): return (state, tile[:, :12].T)]
where the time goes in v2:
time: 85.9 us; the launch traced here: 85.6 us
  Pallas kernels  82.4 us (96%)
  local copies, waits for them, and re-layouts  2.57 us (3%)
    pallas_call x1, Pallas kernels, body(): pl.pallas_call(kernel, out_shape=(jax.ShapeDtypeStruct((OWN, D), F32), ja...  82.4 us
    unnamed x2, local copies, waits for them, and re-layouts  2.57 us

profile of v2, /device:TPU:0, one launch (start us, length us, event | category | flops | bytes accessed | tf_op | source)
XLA Modules:
  0.0 85.6 jit_solution(10154974369169683368)
XLA Ops:
  0.6 82.4 %structure.1 = (f32[8,384]{1,0:T(8,128)}, f32[8,12]{1,0:T(8,128)}) custom-call(f32[8,384]{1,0:T(8,128)} %single_in.1, f32[3,8]{1,0:T(4,128)} %rotation_in.1, f32[3,8]{1,0:T(4,128)} %translation_in.1, s32[1,8]{1,0:T(1,128)} %bitcast.14, s32[1,8]{1,0:T(1,128)} %bitcast.15, f32[1,12]{1,0:T(1,128)} %bitcast.16, bf16[128,128]{1,0:T(8,128)(2,1)} %relpos.1, ...), custom_call_target="tpu_custom_call" | custom-call | tf_op jit(solution)/shard_map/structure/pallas_call | solution.py:697
  83.0 1.3 %copy.20 = f32[8,384]{1,0:T(8,128)} copy(f32[8,384]{1,0:T(8,128)} %get-tuple-element.8) | data formatting | bytes 24576
  84.3 1.3 %copy.21 = f32[12,8]{0,1:T(8,128)} copy(f32[12,8]{0,1:T(8,128)} %bitcast.13) | data formatting | bytes 768

commit v3 on v2

--- a/solution.py
+++ b/solution.py
@@ -88,15 +88,16 @@
 
 
 def kernel(
+    single_hbm, rotation_hbm, translation_hbm, index_hbm, live_hbm, head_hbm, relpos_hbm, gain_hbm,
+    wb_hbm, wframe_hbm, pair_hbm, wsc_hbm, wpt_hbm, wout_hbm, whid_hbm, wback_hbm,
+    single_out, frames_out,
     single_in, rotation_in, translation_in, index_in, live_in, head_in, relpos, gain, wb_in, wframe,
-    pair_hbm, wsc_hbm, wpt_hbm, wout_hbm, whid_hbm, wback_hbm,
-    single_out, frames_out,
     pair_v, bias_v, wsc_f, wpt_f, wout_f, whid_f, wback_f, wfr_f,
     wp_hi, wp_mid, wmix_hi, wmix_mid, wloc_hi, wloc_mid, whid_hi, whid_mid, wback_hi, wback_mid,
     wfr_hi, wfr_mid, wb_s, small, gamma, hmask, centre,
-    send_buf, row_recv, swap_recv, col_recv, sync_send, sync_recv, mix_send, mix_recv,
+    state_f, send_buf, row_recv, swap_recv, col_recv, sync_send, sync_recv, mix_send, mix_recv,
     pts_send, pts_recv,
-    qf, qmask, kf, vcat, idx_b, p_s, m_b, s_b, r_s, pair_s,
+    qf, qmask, kf, vcat, idx_b, p_s, m_b, s_b, r_s, sums_s, pair_s,
     copy_sem, row_ss, row_rs, swap_ss, swap_rs, col_ss, col_rs, sync_ss, sync_rs,
     mix_ss, mix_rs, pts_ss, pts_rs,
 ):
@@ -117,6 +118,34 @@
 
     slot = slot_of(r)
 
+    barrier = pltpu.get_barrier_semaphore()
+    for d in range(1, NC):
+        pl.semaphore_signal(
+            barrier, inc=1, device_id=(r, lax.rem(c + d, NC)), device_id_type=MESH
+        )
+    for d in range(1, NR):
+        pl.semaphore_signal(
+            barrier, inc=1, device_id=(lax.rem(r + d, NR), c), device_id_type=MESH
+        )
+    pl.semaphore_signal(barrier, inc=1, device_id=(from_row, from_col), device_id_type=MESH)
+
+    small_copies = [
+        pltpu.make_async_copy(src, dst, copy_sem.at[6 + k])
+        for k, (src, dst) in enumerate(
+            [
+                (single_hbm, single_in),
+                (rotation_hbm, rotation_in),
+                (translation_hbm, translation_in),
+                (index_hbm, index_in),
+                (live_hbm, live_in),
+                (head_hbm, head_in),
+                (relpos_hbm, relpos),
+                (gain_hbm, gain),
+                (wb_hbm, wb_in),
+                (wframe_hbm, wframe),
+            ]
+        )
+    ]
     copies = [
         pltpu.make_async_copy(src, dst, copy_sem.at[k])
         for k, (src, dst) in enumerate(
@@ -130,19 +159,10 @@
             ]
         )
     ]
-    for cp in copies:
+    for cp in small_copies + copies:
         cp.start()
-
-    barrier = pltpu.get_barrier_semaphore()
-    for d in range(1, NC):
-        pl.semaphore_signal(
-            barrier, inc=1, device_id=(r, lax.rem(c + d, NC)), device_id_type=MESH
-        )
-    for d in range(1, NR):
-        pl.semaphore_signal(
-            barrier, inc=1, device_id=(lax.rem(r + d, NR), c), device_id_type=MESH
-        )
-    pl.semaphore_signal(barrier, inc=1, device_id=(from_row, from_col), device_id_type=MESH)
+    for cp in small_copies:
+        cp.wait()
 
     small[...] = jnp.zeros_like(small)
     entries = rotation_entries(rotation_in[0:1], rotation_in[1:2], rotation_in[2:3])
@@ -156,8 +176,27 @@
     positive = jnp.maximum(head, 0.0) + jnp.log1p(jnp.exp(-jnp.abs(head)))
     small[14:15, 0:H] = positive * (math.sqrt(2.0 / (9.0 * PQ)) / 2.0)
     turned = small[...].T
-    send_buf[0, :, 0:D] = single_in[...]
-    send_buf[0, :, D:] = jnp.where(lane_iota(OWN) < 14, pad_lanes(turned[0:OWN]), 0.0)
+    state_f[:, 0:D] = single_in[...]
+    state_f[:, D:] = pad_lanes(jnp.concatenate([turned[0:OWN]] * 3, axis=1))
+
+    def pack(single, frames):
+        at = lane_iota(OWN)
+        hi, mid = split2(frames)
+        lo = (frames - hi.astype(F32) - mid.astype(F32)).astype(BF16)
+        pieces = jnp.where(
+            at < 16,
+            hi.astype(F32),
+            jnp.where(at < 32, mid.astype(F32), jnp.where(at < 48, lo.astype(F32), 0.0)),
+        )
+        return jnp.concatenate([single.astype(BF16), pieces.astype(BF16)], axis=1)
+
+    def unpack(blocks):
+        rows = blocks.astype(F32).reshape(blocks.shape[0] * OWN, SW)
+        f = rows[:, D:]
+        f = f + pltpu.roll(f, 112, 1) + pltpu.roll(f, 96, 1)
+        return rows[:, :D].astype(BF16), f
+
+    send_buf[0] = pack(state_f[:, 0:D], state_f[:, D:])
 
     lane = lane_iota(HP)
     head_row = lax.broadcasted_iota(jnp.int32, (HP, 128), 0)
@@ -317,10 +356,10 @@
         return hi, mid, lo
 
     def query_features(it):
-        s = row_recv[it].reshape(ROWS, SW)
-        y = dot3(s[:, :D], wp_hi[:, :QW], wp_mid[:, :QW])
+        s, f = unpack(row_recv[it])
+        y = mm(s, wp_hi[:, :QW]) + mm(s, wp_mid[:, :QW])
         qf[:, 0:256] = y[:, :256]
-        comps = to_global(s[:, D:], y[:, 256:], 96)
+        comps = to_global(f, y[:, 256:], 96)
         squares = square_terms(comps)
         lane = lane_iota(ROWS)
         for a in range(3):
@@ -344,12 +383,9 @@
         lax.fori_loop(0, ROWS // 4, spread, 0)
 
     def key_features(it):
-        s = col_recv[it].reshape(COLS, SW)
-        hi, mid = split2(s[:, :D])
-        w_hi, w_mid = wp_hi[:, QW:], wp_mid[:, QW:]
-        y = mm(hi, w_hi) + mm(mid, w_hi) + mm(hi, w_mid)
+        s, f = unpack(col_recv[it])
+        y = mm(s, wp_hi[:, QW : 2 * QW]) + mm(s, wp_mid[:, QW : 2 * QW])
         kf[:, 0:256] = y[:, :256].astype(BF16)
-        f = s[:, D:]
         comps = to_global(f, y[:, 256:QW], 96)
         squares = square_terms(comps)
         lane = lane_iota(COLS)
@@ -363,9 +399,13 @@
             ).astype(BF16)
             ones = jnp.where((lane >= 96) & (lane < 96 + H), 1.0, zero)
             kf[:, 640 + 128 * a : 768 + 128 * a] = jnp.where(lane < 48, hi, ones).astype(BF16)
-        vcat[0:COLS, 0:256] = y[:, QW : QW + 256].astype(BF16)
+
+    def value_features(it):
+        s, f = unpack(col_recv[it])
+        y = mm(s, wp_hi[:, 2 * QW :]) + mm(s, wp_mid[:, 2 * QW :])
+        vcat[0:COLS, 0:256] = y[:, :256].astype(BF16)
         vcat[COLS:, 0:256] = jnp.zeros((COLS, 256), BF16)
-        values = to_global(f, y[:, QW + 256 :], 96)
+        values = to_global(f, y[:, 256:], 96)
         for a in range(3):
             hi, mid = split2(values[a])
             at = 256 + 128 * a
@@ -374,8 +414,8 @@
 
     def prepare_pair():
         copies[2].wait()
-        fq = row_recv[0].reshape(ROWS, SW)[:, D:]
-        fk = col_recv[0].reshape(COLS, SW)[:, D:]
+        fq = unpack(row_recv[0])[1]
+        fk = unpack(col_recv[0])[1]
         idx_b[0:ROWS] = column(fq, 12)
         idx_b[ROWS:] = column(fq, 13)
         key_index = column(fk, 12)
@@ -448,6 +488,11 @@
             sync_copy(it, lax.rem(c + d, NC), c).start()
         sync_recv[it, c] = sync_send[it]
 
+        @pl.when(it == 0)
+        def _():
+            prepare_weights()
+
+        value_features(it)
         for i in range(ROWS):
             part = pl.ds(i * HP, HP)
             pair_s[part, :] = mm(p_s[part, 0:128], pair_v[i])
@@ -457,6 +502,26 @@
             y = mm(p_s[part, :], values)
             for t in range(5):
                 r_s[t, part, :] = y[:, 128 * t : 128 * t + 128]
+
+        wide = lane_iota(ROWS)
+
+        def layout_of(t):
+            if t == 0:
+                return range(0, 8), 0, C
+            if t == 1:
+                return range(8, 12), 8, C
+            return range(0, H), 0, PV
+
+        def by_head(t, piece):
+            heads, first, size = layout_of(t)
+            out = jnp.zeros((ROWS, 128), F32)
+            for h in heads:
+                lo = (h - first) * size
+                out = jnp.where((wide >= lo) & (wide < lo + size), piece(h), out)
+            return out
+
+        for t in range(5):
+            sums_s[t] = by_head(t, lambda h: r_s[t, pl.ds(h, ROWS, stride=HP), :])
 
         with jax.named_scope("wait_sync"):
             for d in range(1, NC):
@@ -475,27 +540,16 @@
                 jnp.concatenate([column(factor, g * HP + h) for g in range(8)], axis=0)
             )
 
-        wide = lane_iota(ROWS)
-        tiles = {}
-        for t in (2, 3, 4, 0, 1):
-            out = jnp.zeros((ROWS, 128), F32)
-            if t == 0:
-                heads, first, size = range(0, 8), 0, C
-            elif t == 1:
-                heads, first, size = range(8, 12), 8, C
-            else:
-                heads, first, size = range(0, H), 0, PV
-            for h in heads:
-                part = r_s[t, pl.ds(h, ROWS, stride=HP), :] * scale[h]
-                lo = (h - first) * size
-                out = jnp.where((wide >= lo) & (wide < lo + size), part, out)
-            tiles[t] = out
+        scale_points = by_head(2, lambda h: scale[h])
         for a in range(3):
-            pts_send[it, :, :, 128 * a : 128 * a + 128] = tiles[2 + a].reshape(NC, OWN, 128)
+            pts_send[it, :, :, 128 * a : 128 * a + 128] = (sums_s[2 + a] * scale_points).reshape(
+                NC, OWN, 128
+            )
         for d in range(1, NC):
             pts_copy(it, lax.rem(c + d, NC), c).start()
         pairs = [pair_s[pl.ds(h, ROWS, stride=HP), :] * scale[h] for h in range(H)]
-        mixed_in = jnp.concatenate([tiles[0], tiles[1]] + pairs, axis=1)
+        scalars = [sums_s[t] * by_head(t, lambda h: scale[h]) for t in range(2)]
+        mixed_in = jnp.concatenate(scalars + pairs, axis=1)
         mixed = dot3(mixed_in, wmix_hi[...], wmix_mid[...])
         mix_send[it] = mixed.reshape(NC, OWN, D)
         for d in range(1, NC):
@@ -511,9 +565,8 @@
         points = pts_recv[it, 0]
         for k in range(1, NC):
             points = points + pts_recv[it, k]
-        state = send_buf[it]
-        frames = state[:, D:]
-        single = state[:, :D]
+        frames = state_f[:, D:]
+        single = state_f[:, :D]
         moved = [points[:, 128 * a : 128 * a + 128] - column(frames, 9 + a) for a in range(3)]
         local = [
             column(frames, a) * moved[0]
@@ -553,7 +606,7 @@
             + column(frames, 9 + left)
             for left in range(3)
         ]
-        lane = lane_iota(OWN)
+        lane = lax.rem(lane_iota(OWN), 16)
         out = frames
         for k, value in enumerate(new):
             out = jnp.where(lane == k, value, out)
@@ -573,10 +626,6 @@
             for d in range(1, NR):
                 col_copy(it, lax.rem(r + d, NR), slot).start()
             col_recv[it, slot] = swap_recv[it]
-
-            @pl.when(it == 0)
-            def _():
-                prepare_weights()
 
         with jax.named_scope("wait_row"):
             for d in range(1, NC):
@@ -603,8 +652,9 @@
 
             @pl.when(it < ITERS - 1)
             def _():
-                send_buf[it + 1, :, 0:D] = single
-                send_buf[it + 1, :, D:] = frames
+                send_buf[it + 1] = pack(single, frames)
+                state_f[:, 0:D] = single
+                state_f[:, D:] = frames
 
             @pl.when(it == ITERS - 1)
             def _():
@@ -626,6 +676,11 @@
     lax.fori_loop(0, ITERS, iteration, 0)
 
 
+def hand_over(state, frames, state_out, frames_out):
+    state_out[...] = state[...]
+    frames_out[...] = frames[...]
+
+
 def body(
     pair, relpos, pair_gain, bias_weight, single, rotation_params, translation, residue_index,
     residue_mask, w_scalar, w_points, head_weights, w_out, w_hidden, w_back, w_frame,
@@ -635,6 +690,16 @@
     V = pltpu.VMEM
     dma = pltpu.SemaphoreType.DMA
     scratch = [
+        V((OWN, D), F32),
+        V((3, OWN), F32),
+        V((3, OWN), F32),
+        V((1, OWN), jnp.int32),
+        V((1, OWN), jnp.int32),
+        V((1, H), F32),
+        V((128, 128), BF16),
+        V((1, 128), F32),
+        V((H, 128), BF16),
+        V((6, D), F32),
         V((ROWS, COLS, 128), BF16),
         V((ROWS * HP, 128), F32),
         V((576, D), F32),
@@ -660,10 +725,11 @@
         V((1, 128), F32),
         V((HP, FW), F32),
         V((3 * 128, 128), BF16),
-        V((ITERS, OWN, SW), F32),
-        V((ITERS, NC, OWN, SW), F32),
-        V((ITERS, OWN, SW), F32),
-        V((ITERS, NR, OWN, SW), F32),
+        V((OWN, SW), F32),
+        V((ITERS, OWN, SW), BF16),
+        V((ITERS, NC, OWN, SW), BF16),
+        V((ITERS, OWN, SW), BF16),
+        V((ITERS, NR, OWN, SW), BF16),
         V((ITERS, 16, 128), F32),
         V((ITERS, NC, 16, 128), F32),
         V((ITERS, NC, OWN, D), F32),
@@ -679,8 +745,9 @@
         V((ROWS * HP, 128), F32),
         V((ROWS * HP, 128), F32),
         V((5, ROWS * HP, 128), F32),
+        V((5, ROWS, 128), F32),
         V((ROWS * HP, 128), F32),
-        dma((6,)),
+        dma((16,)),
         dma((NC,)),
         dma((ITERS, NC)),
         dma,
@@ -700,7 +767,7 @@
             jax.ShapeDtypeStruct((OWN, D), F32),
             jax.ShapeDtypeStruct((OWN, 12), F32),
         ),
-        in_specs=[vmem] * 10 + [anyspace] * 6,
+        in_specs=[anyspace] * 16,
         out_specs=(vmem, vmem),
         scratch_shapes=scratch,
         compiler_params=pltpu.CompilerParams(
@@ -713,6 +780,17 @@
         pair_gain.reshape(1, 128), bias_weight.T, w_frame.T,
         pair, w_scalar.T, w_points.T, w_out, w_hidden, w_back,
     )
+    state, frames = pl.pallas_call(
+        hand_over,
+        out_shape=(
+            jax.ShapeDtypeStruct((OWN, D), F32),
+            jax.ShapeDtypeStruct((OWN, 12), F32),
+        ),
+        in_specs=[vmem, vmem],
+        out_specs=(vmem, vmem),
+        compiler_params=pltpu.CompilerParams(vmem_limit_bytes=1024 * 1024),
+        name="hand_over",
+    )(state, frames)
     return state, frames.T
 
 

time: 85.9 us -> 80.7 us (0.939)
  Pallas kernels: 82.4 us -> 78.4 us
  local copies, waits for them, and re-layouts: 2.57 us -> 1.38 us
    pallas_call x1, Pallas kernels: 82.4 us -> 77.8 us  [body(): pl.pallas_call(kernel, out_shape=(jax.ShapeDtypeStruct((OWN, D), F32), ja...]
    unnamed x2 -> x4, local copies, waits for them, and re-layouts: 2.57 us -> 1.38 us
where the time goes in v3:
time: 80.7 us; the launch traced here: 80.4 us
  Pallas kernels  78.4 us (97%)
  local copies, waits for them, and re-layouts  1.38 us (2%)
    pallas_call x1, Pallas kernels, body(): pl.pallas_call(kernel, out_shape=(jax.ShapeDtypeStruct((OWN, D), F32), ja...  77.8 us

profile of v3, /device:TPU:0, one launch (start us, length us, event | category | flops | bytes accessed | tf_op | source)
XLA Modules:
  0.0 80.4 jit_solution(16304618174537663543)
XLA Ops:
  0.6 77.8 %structure.1 = (f32[8,384]{1,0:T(8,128)}, f32[8,12]{1,0:T(8,128)}) custom-call(f32[8,384]{1,0:T(8,128)} %single_hbm.1, f32[3,8]{1,0:T(4,128)} %rotation_hbm.1, f32[3,8]{1,0:T(4,128)} %translation_hbm.1, s32[1,8]{1,0:T(1,128)} %bitcast.13, s32[1,8]{1,0:T(1,128)} %bitcast.14, f32[1,12]{1,0:T(1,128)} %bitcast.15, bf16[128,128]{1,0:T(8,128)(2,1)} %relpos_hbm.1, ...), custom_call_target="tpu_custom_call" | custom-call | tf_op jit(solution)/shard_map/structure/pallas_call | solution.py:764
  78.4 0.0 copy-start
  78.4 0.7 copy-done
  79.1 0.0 copy-start.1
  79.1 0.7 copy-done.1
  79.8 0.6 hand_over.1
Async XLA Ops:
  78.4 0.7 copy-start
  79.1 0.7 copy-start.1

commit v4 on v3

--- a/solution.py
+++ b/solution.py
@@ -96,10 +96,10 @@
     wp_hi, wp_mid, wmix_hi, wmix_mid, wloc_hi, wloc_mid, whid_hi, whid_mid, wback_hi, wback_mid,
     wfr_hi, wfr_mid, wb_s, small, gamma, hmask, centre,
     state_f, send_buf, row_recv, swap_recv, col_recv, sync_send, sync_recv, mix_send, mix_recv,
-    pts_send, pts_recv,
+    pts_send, pts_recv, idx_recv, key_idx,
     qf, qmask, kf, vcat, idx_b, p_s, m_b, s_b, r_s, sums_s, pair_s,
     copy_sem, row_ss, row_rs, swap_ss, swap_rs, col_ss, col_rs, sync_ss, sync_rs,
-    mix_ss, mix_rs, pts_ss, pts_rs,
+    mix_ss, mix_rs, pts_ss, pts_rs, idx_ss, idx_rs,
 ):
     r = lax.axis_index("row")
     c = lax.axis_index("col")
@@ -117,16 +117,25 @@
         return lax.rem(row, 2) * 8 + (row // 8) * 4 + lax.rem(2 * x + 6 - lax.rem(row // 2, 4), 4)
 
     slot = slot_of(r)
+    near = (r >= 2 * c - 1) & (r <= 2 * c + 2)
+    diagonal = r // 2 == c
+
+    row_peers = [
+        lax.rem(y_lo + dy, 2) * 4 + lax.rem(x + dx, 4)
+        for dy, dx in ((1, 2), (1, 1), (1, 3), (0, 2), (1, 0), (0, 1), (0, 3))
+    ]
+    col_peers = [
+        lax.rem(y_hi + dy, 2) * 8 + lax.rem(z + dz, 4) * 2 + lax.rem(core + dc, 2)
+        for dy, dz in ((1, 2), (1, 1), (1, 3), (1, 0), (0, 2), (0, 1), (0, 3), (0, 0))
+        for dc in (0, 1)
+        if (dy, dz, dc) != (0, 0, 0)
+    ]
 
     barrier = pltpu.get_barrier_semaphore()
-    for d in range(1, NC):
-        pl.semaphore_signal(
-            barrier, inc=1, device_id=(r, lax.rem(c + d, NC)), device_id_type=MESH
-        )
-    for d in range(1, NR):
-        pl.semaphore_signal(
-            barrier, inc=1, device_id=(lax.rem(r + d, NR), c), device_id_type=MESH
-        )
+    for peer in col_peers:
+        pl.semaphore_signal(barrier, inc=1, device_id=(peer, c), device_id_type=MESH)
+    for peer in row_peers:
+        pl.semaphore_signal(barrier, inc=1, device_id=(r, peer), device_id_type=MESH)
     pl.semaphore_signal(barrier, inc=1, device_id=(from_row, from_col), device_id_type=MESH)
 
     small_copies = [
@@ -246,6 +255,57 @@
             device_id_type=MESH,
         )
 
+    def idx_copy(peer, k, at):
+        return pltpu.make_async_remote_copy(
+            src_ref=row_recv.at[0, :, :, D:SW],
+            dst_ref=idx_recv.at[at],
+            send_sem=idx_ss.at[k],
+            recv_sem=idx_rs.at[at],
+            device_id=(peer, c),
+            device_id_type=MESH,
+        )
+
+    idx_targets = (
+        (diagonal, r + 1 - 2 * core),
+        (diagonal & (c > 0), lax.rem(2 * c + 15, 16)),
+        (diagonal & (c < NC - 1), lax.rem(2 * c + 2, 16)),
+    )
+
+    def send_numbers():
+        for k, (needed, peer) in enumerate(idx_targets):
+
+            @pl.when(needed)
+            def _(k=k, peer=peer):
+                idx_copy(peer, k, core).start()
+
+        @pl.when(diagonal)
+        def _():
+            idx_recv[core] = row_recv[0, :, :, D:SW]
+
+    def key_numbers():
+        @pl.when(diagonal)
+        def _():
+            idx_copy(r, 0, 1 - core).wait_recv()
+
+        @pl.when(near & jnp.logical_not(diagonal))
+        def _():
+            idx_copy(r, 0, 0).wait_recv()
+            idx_copy(r, 0, 1).wait_recv()
+
+        @pl.when(near)
+        def _():
+            f = idx_recv[...].astype(F32).reshape(COLS, 128)
+            f = f + pltpu.roll(f, 112, 1) + pltpu.roll(f, 96, 1)
+            key_idx[...] = column(f, 12)
+
+        @pl.when(jnp.logical_not(near) & (c > r // 2))
+        def _():
+            key_idx[...] = jnp.full((COLS, 128), 1e6, F32)
+
+        @pl.when(jnp.logical_not(near) & (c < r // 2))
+        def _():
+            key_idx[...] = jnp.full((COLS, 128), -1e6, F32)
+
     def sync_copy(it, peer, at):
         return pltpu.make_async_remote_copy(
             src_ref=sync_send.at[it],
@@ -278,8 +338,8 @@
 
     def start_exchange(it):
         swap_copy(it).start()
-        for d in range(1, NC):
-            row_copy(it, lax.rem(c + d, NC), c).start()
+        for peer in row_peers:
+            row_copy(it, peer, c).start()
         row_recv[it, c] = send_buf[it]
 
     def prepare_projection():
@@ -415,11 +475,9 @@
     def prepare_pair():
         copies[2].wait()
         fq = unpack(row_recv[0])[1]
-        fk = unpack(col_recv[0])[1]
         idx_b[0:ROWS] = column(fq, 12)
         idx_b[ROWS:] = column(fq, 13)
-        key_index = column(fk, 12)
-        key_live = fk.T[13:14, :]
+        key_index = key_idx[...]
         shape = (COLS, 128)
         lane = lax.broadcasted_iota(jnp.int32, shape, 1).astype(F32) - 64.0
         same = lax.broadcasted_iota(jnp.int32, shape, 0) == lax.broadcasted_iota(jnp.int32, shape, 1)
@@ -449,59 +507,69 @@
                 bias = lax.dot_general(
                     project, normed, (((1,), (1,)), ((), ())), preferred_element_type=F32
                 )
-                live = key_live * idx_b[pl.ds(ROWS + first + u, 1), :] > 0.5
+                live = idx_b[pl.ds(ROWS + first + u, 1), :] > 0.5
                 at = pl.multiple_of((first + u) * HP, HP)
                 bias_v[pl.ds(at, HP), :] = jnp.where(live, bias * THIRD, DEAD)
             return carry
 
         lax.fori_loop(0, ROWS // step, prepare, 0)
 
-    def attend(it):
-        keys = kf[...]
-        rows = 256
-        for k in range(ROWS * HP // rows):
-            part = pl.ds(k * rows, rows)
-            acc = lax.dot_general(
-                qmask[part, :], keys, (((1,), (1,)), ((), ())), preferred_element_type=F32
-            )
-            bias = bias_v[part, :]
-            logits = jnp.where(bias > -1e38, acc * (THIRD / math.sqrt(C)) + bias, MASKED_LOGIT)
-            top = jnp.max(logits, axis=-1, keepdims=True)
-            p = jnp.exp(logits - top).astype(BF16)
-            m_b[part, :] = jnp.broadcast_to(top, (rows, 128))
-            total = jnp.sum(p.astype(F32), axis=-1, keepdims=True)
-            s_b[part, :] = jnp.broadcast_to(total, (rows, 128))
-            p_s[part, 0:128] = p
-            p_s[part, 128:256] = p
-
-        lane = lane_iota(8)
-        tops = jnp.zeros((8, 128), F32)
-        sums = jnp.zeros((8, 128), F32)
-        for g in range(8):
-            for h in range(HP):
-                src = pl.ds(8 * HP * g + h, 8, stride=HP)
-                tops = jnp.where(lane == g * HP + h, m_b[src, :], tops)
-                sums = jnp.where(lane == g * HP + h, s_b[src, :], sums)
-        sync_send[it, 0:8] = tops
-        sync_send[it, 8:16] = sums
-        for d in range(1, NC):
-            sync_copy(it, lax.rem(c + d, NC), c).start()
-        sync_recv[it, c] = sync_send[it]
-
-        @pl.when(it == 0)
-        def _():
-            prepare_weights()
-
-        value_features(it)
-        for i in range(ROWS):
-            part = pl.ds(i * HP, HP)
-            pair_s[part, :] = mm(p_s[part, 0:128], pair_v[i])
-        values = vcat[...]
+    def mask_keys():
+        live = unpack(col_recv[0])[1].T[13:14, :] > 0.5
         for k in range(4):
             part = pl.ds(k * 256, 256)
-            y = mm(p_s[part, :], values)
-            for t in range(5):
-                r_s[t, part, :] = y[:, 128 * t : 128 * t + 128]
+            bias_v[part, :] = jnp.where(live, bias_v[part, :], DEAD)
+
+    def attend(it):
+        with jax.named_scope("logits"):
+            keys = kf[...]
+            rows = 256
+            for k in range(ROWS * HP // rows):
+                part = pl.ds(k * rows, rows)
+                acc = lax.dot_general(
+                    qmask[part, :], keys, (((1,), (1,)), ((), ())), preferred_element_type=F32
+                )
+                bias = bias_v[part, :]
+                logits = jnp.where(bias > -1e38, acc * (THIRD / math.sqrt(C)) + bias, MASKED_LOGIT)
+                top = jnp.max(logits, axis=-1, keepdims=True)
+                p = jnp.exp(logits - top).astype(BF16)
+                m_b[part, :] = jnp.broadcast_to(top, (rows, 128))
+                total = jnp.sum(p.astype(F32), axis=-1, keepdims=True)
+                s_b[part, :] = jnp.broadcast_to(total, (rows, 128))
+                p_s[part, 0:128] = p
+                p_s[part, 128:256] = p
+
+        with jax.named_scope("pack"):
+            lane = lane_iota(8)
+            tops = jnp.zeros((8, 128), F32)
+            sums = jnp.zeros((8, 128), F32)
+            for g in range(8):
+                for h in range(HP):
+                    src = pl.ds(8 * HP * g + h, 8, stride=HP)
+                    tops = jnp.where(lane == g * HP + h, m_b[src, :], tops)
+                    sums = jnp.where(lane == g * HP + h, s_b[src, :], sums)
+            sync_send[it, 0:8] = tops
+            sync_send[it, 8:16] = sums
+            for peer in row_peers:
+                sync_copy(it, peer, c).start()
+            sync_recv[it, c] = sync_send[it]
+
+        with jax.named_scope("values"):
+            @pl.when(it == 0)
+            def _():
+                prepare_weights()
+
+            value_features(it)
+        with jax.named_scope("sums"):
+            for i in range(ROWS):
+                part = pl.ds(i * HP, HP)
+                pair_s[part, :] = mm(p_s[part, 0:128], pair_v[i])
+            values = vcat[...]
+            for k in range(4):
+                part = pl.ds(k * 256, 256)
+                y = mm(p_s[part, :], values)
+                for t in range(5):
+                    r_s[t, part, :] = y[:, 128 * t : 128 * t + 128]
 
         wide = lane_iota(ROWS)
 
@@ -520,12 +588,12 @@
                 out = jnp.where((wide >= lo) & (wide < lo + size), piece(h), out)
             return out
 
-        for t in range(5):
-            sums_s[t] = by_head(t, lambda h: r_s[t, pl.ds(h, ROWS, stride=HP), :])
+        with jax.named_scope("select"):
+            for t in range(5):
+                sums_s[t] = by_head(t, lambda h: r_s[t, pl.ds(h, ROWS, stride=HP), :])
 
         with jax.named_scope("wait_sync"):
-            for d in range(1, NC):
-                peer = lax.rem(c + d, NC)
+            for peer in row_peers:
                 sync_copy(it, peer, peer).wait_recv()
         all_tops = [sync_recv[it, k, 0:8] for k in range(NC)]
         top = functools.reduce(jnp.maximum, all_tops)
@@ -534,33 +602,34 @@
             total = total + sync_recv[it, k, 8:16] * jnp.exp(all_tops[k] - top)
         factor = jnp.exp(tops - top) / total
 
-        scale = []
-        for h in range(H):
-            scale.append(
-                jnp.concatenate([column(factor, g * HP + h) for g in range(8)], axis=0)
-            )
-
-        scale_points = by_head(2, lambda h: scale[h])
-        for a in range(3):
-            pts_send[it, :, :, 128 * a : 128 * a + 128] = (sums_s[2 + a] * scale_points).reshape(
-                NC, OWN, 128
-            )
-        for d in range(1, NC):
-            pts_copy(it, lax.rem(c + d, NC), c).start()
-        pairs = [pair_s[pl.ds(h, ROWS, stride=HP), :] * scale[h] for h in range(H)]
-        scalars = [sums_s[t] * by_head(t, lambda h: scale[h]) for t in range(2)]
-        mixed_in = jnp.concatenate(scalars + pairs, axis=1)
-        mixed = dot3(mixed_in, wmix_hi[...], wmix_mid[...])
-        mix_send[it] = mixed.reshape(NC, OWN, D)
-        for d in range(1, NC):
-            mix_copy(it, lax.rem(c + d, NC), c).start()
-        pts_recv[it, c] = pts_send[it, c]
-        mix_recv[it, c] = mix_send[it, c]
+        with jax.named_scope("factor"):
+            scale = []
+            for h in range(H):
+                scale.append(
+                    jnp.concatenate([column(factor, g * HP + h) for g in range(8)], axis=0)
+                )
+
+            scale_points = by_head(2, lambda h: scale[h])
+            for a in range(3):
+                pts_send[it, :, :, 128 * a : 128 * a + 128] = (sums_s[2 + a] * scale_points).reshape(
+                    NC, OWN, 128
+                )
+            for peer in row_peers:
+                pts_copy(it, peer, c).start()
+        with jax.named_scope("mix"):
+            pairs = [pair_s[pl.ds(h, ROWS, stride=HP), :] * scale[h] for h in range(H)]
+            scalars = [sums_s[t] * by_head(t, lambda h: scale[h]) for t in range(2)]
+            mixed_in = jnp.concatenate(scalars + pairs, axis=1)
+            mixed = dot3(mixed_in, wmix_hi[...], wmix_mid[...])
+            mix_send[it] = mixed.reshape(NC, OWN, D)
+            for peer in row_peers:
+                mix_copy(it, peer, c).start()
+            pts_recv[it, c] = pts_send[it, c]
+            mix_recv[it, c] = mix_send[it, c]
 
     def advance(it):
         with jax.named_scope("wait_pts"):
-            for d in range(1, NC):
-                peer = lax.rem(c + d, NC)
+            for peer in row_peers:
                 pts_copy(it, peer, peer).wait_recv()
         points = pts_recv[it, 0]
         for k in range(1, NC):
@@ -581,8 +650,7 @@
         feats = jnp.concatenate([jnp.where(keep, x, 0.0) for x in local + [lengths]], axis=1)
         single = single + dot3(feats, wloc_hi[...], wloc_mid[...])
         with jax.named_scope("wait_mix"):
-            for d in range(1, NC):
-                peer = lax.rem(c + d, NC)
+            for peer in row_peers:
                 mix_copy(it, peer, peer).wait_recv()
         for k in range(NC):
             single = single + mix_recv[it, k]
@@ -623,30 +691,38 @@
         with jax.named_scope("wait_swap"):
             swap_copy(it).wait_recv()
         with jax.named_scope("send_col"):
-            for d in range(1, NR):
-                col_copy(it, lax.rem(r + d, NR), slot).start()
+            for peer in col_peers:
+                col_copy(it, peer, slot).start()
             col_recv[it, slot] = swap_recv[it]
 
         with jax.named_scope("wait_row"):
-            for d in range(1, NC):
-                peer = lax.rem(c + d, NC)
+            for peer in row_peers:
                 row_copy(it, peer, peer).wait_recv()
         with jax.named_scope("query"):
+
+            @pl.when(it == 0)
+            def _():
+                send_numbers()
+
             query_features(it)
+        with jax.named_scope("prep_pair"):
+
+            @pl.when(it == 0)
+            def _():
+                key_numbers()
+                prepare_pair()
+
         with jax.named_scope("wait_col"):
-            for d in range(1, NR):
-                peer = lax.rem(r + d, NR)
+            for peer in col_peers:
                 col_copy(it, peer, slot_of(peer)).wait_recv()
         with jax.named_scope("key"):
             key_features(it)
-        with jax.named_scope("prep_pair"):
 
             @pl.when(it == 0)
             def _():
-                prepare_pair()
-
-        with jax.named_scope("attend"):
-            attend(it)
+                mask_keys()
+
+        attend(it)
         with jax.named_scope("advance"):
             single, frames = advance(it)
 
@@ -663,17 +739,21 @@
 
         with jax.named_scope("wait_send"):
             swap_copy(it).wait_send()
-            for d in range(1, NC):
-                peer = lax.rem(c + d, NC)
+            for peer in row_peers:
                 row_copy(it, peer, c).wait_send()
                 sync_copy(it, peer, c).wait_send()
                 pts_copy(it, peer, c).wait_send()
                 mix_copy(it, peer, c).wait_send()
-            for d in range(1, NR):
-                col_copy(it, lax.rem(r + d, NR), slot).wait_send()
+            for peer in col_peers:
+                col_copy(it, peer, slot).wait_send()
         return carry
 
     lax.fori_loop(0, ITERS, iteration, 0)
+    for k, (needed, peer) in enumerate(idx_targets):
+
+        @pl.when(needed)
+        def _(k=k, peer=peer):
+            idx_copy(peer, k, core).wait_send()
 
 
 def hand_over(state, frames, state_out, frames_out):
@@ -736,6 +816,8 @@
         V((ITERS, NC, OWN, D), F32),
         V((ITERS, NC, OWN, D), F32),
         V((ITERS, NC, OWN, D), F32),
+        V((2, NC, OWN, 128), BF16),
+        V((COLS, 128), F32),
         V((ROWS, FW), F32),
         V((ROWS * HP, FW), BF16),
         V((COLS, FW), BF16),
@@ -760,6 +842,8 @@
         dma((ITERS, NC)),
         dma((NC,)),
         dma((ITERS, NC)),
+        dma((3,)),
+        dma((2,)),
     ]
     state, frames = pl.pallas_call(
         kernel,
@@ -771,7 +855,7 @@
         out_specs=(vmem, vmem),
         scratch_shapes=scratch,
         compiler_params=pltpu.CompilerParams(
-            collective_id=0, has_side_effects=True, vmem_limit_bytes=60 * 1024 * 1024
+            collective_id=0, has_side_effects=True, vmem_limit_bytes=62 * 1024 * 1024
         ),
         name="structure",
     )(
@@ -788,7 +872,7 @@
         ),
         in_specs=[vmem, vmem],
         out_specs=(vmem, vmem),
-        compiler_params=pltpu.CompilerParams(vmem_limit_bytes=1024 * 1024),
+        compiler_params=pltpu.CompilerParams(vmem_limit_bytes=62 * 1024 * 1024),
         name="hand_over",
     )(state, frames)
     return state, frames.T

time: 80.7 us -> 78 us (0.967)
  local copies, waits for them, and re-layouts: 1.38 us -> 0 us
  Pallas kernels: 78.4 us -> 77.1 us
    pallas_call x1, Pallas kernels: 77.8 us -> 75.8 us  [body(): pl.pallas_call(kernel, out_shape=(jax.ShapeDtypeStruct((OWN, D), F32), ja...]
    unnamed x4 -> x0, local copies, waits for them, and re-layouts: 1.38 us -> none
where the time goes in v4:
time: 78 us; the launch traced here: 77.8 us
  Pallas kernels  77.1 us (99%)
    pallas_call x1, Pallas kernels, body(): pl.pallas_call(kernel, out_shape=(jax.ShapeDtypeStruct((OWN, D), F32), ja...  75.8 us

profile of v4, /device:TPU:0, one launch (start us, length us, event | category | flops | bytes accessed | tf_op | source)
XLA Modules:
  0.0 77.8 jit_solution(13033269205717738452)
XLA Ops:
  0.6 75.8 %structure.1 = (f32[8,384]{1,0:T(8,128)}, f32[8,12]{1,0:T(8,128)}) custom-call(f32[8,384]{1,0:T(8,128)} %single_hbm.1, f32[3,8]{1,0:T(4,128)} %rotation_hbm.1, f32[3,8]{1,0:T(4,128)} %translation_hbm.1, s32[1,8]{1,0:T(1,128)} %bitcast.13, s32[1,8]{1,0:T(1,128)} %bitcast.14, f32[1,12]{1,0:T(1,128)} %bitcast.15, bf16[128,128]{1,0:T(8,128)(2,1)} %relpos_hbm.1, ...), custom_call_target="tpu_custom_call" | custom-call | tf_op jit(solution)/shard_map/structure/pallas_call | solution.py:848
  76.4 1.3 %hand_over.1 = (f32[8,384]{1,0:T(8,128)}, f32[8,12]{1,0:T(8,128)}) custom-call(f32[8,384]{1,0:T(8,128)} %get-tuple-element.6.state, f32[8,12]{1,0:T(8,128)} %get-tuple-element.7.frames), custom_call_target="tpu_custom_call" | custom-call | tf_op jit(solution)/shard_map/hand_over/pallas_call | solution.py:867

commit v5 on v4

--- a/solution.py
+++ b/solution.py
@@ -22,10 +22,8 @@
 NR = 16
 NC = 8
 SW = 512
-RW = 768
 QW = 640
 FW = 1024
-MIXW = 1792
 
 NORM_EPSILON = 1e-05
 MASKED_LOGIT = -100000.0
@@ -95,11 +93,11 @@
     pair_v, bias_v, wsc_f, wpt_f, wout_f, whid_f, wback_f, wfr_f,
     wp_hi, wp_mid, wmix_hi, wmix_mid, wloc_hi, wloc_mid, whid_hi, whid_mid, wback_hi, wback_mid,
     wfr_hi, wfr_mid, wb_s, small, gamma, hmask, centre,
-    state_f, send_buf, row_recv, swap_recv, col_recv, sync_send, sync_recv, mix_send, mix_recv,
-    pts_send, pts_recv, idx_recv, key_idx,
-    qf, qmask, kf, vcat, idx_b, p_s, m_b, s_b, r_s, sums_s, pair_s,
-    copy_sem, row_ss, row_rs, swap_ss, swap_rs, col_ss, col_rs, sync_ss, sync_rs,
-    mix_ss, mix_rs, pts_ss, pts_rs, idx_ss, idx_rs,
+    state_f, send_buf, row_recv, swap_recv, col_recv, top_send, top_recv, pair_send, pair_recv,
+    val_send, val_recv, idx_recv, key_idx,
+    qf, qmask, kf, vcat, idx_b, p_s, m_b, s_b, r_s, pair_s,
+    copy_sem, row_ss, row_rs, swap_ss, swap_rs, col_ss, col_rs, top_ss, top_rs,
+    pair_ss, pair_rs, val_ss, val_rs, idx_ss, idx_rs,
 ):
     r = lax.axis_index("row")
     c = lax.axis_index("col")
@@ -306,32 +304,32 @@
         def _():
             key_idx[...] = jnp.full((COLS, 128), -1e6, F32)
 
-    def sync_copy(it, peer, at):
+    def top_copy(it, peer, at):
         return pltpu.make_async_remote_copy(
-            src_ref=sync_send.at[it],
-            dst_ref=sync_recv.at[it, at],
-            send_sem=sync_ss.at[peer],
-            recv_sem=sync_rs.at[it, at],
+            src_ref=top_send.at[it, peer],
+            dst_ref=top_recv.at[it, at],
+            send_sem=top_ss.at[peer],
+            recv_sem=top_rs.at[it, at],
             device_id=(r, peer),
             device_id_type=MESH,
         )
 
-    def mix_copy(it, peer, at):
+    def pair_copy(it, peer, at):
         return pltpu.make_async_remote_copy(
-            src_ref=mix_send.at[it, peer],
-            dst_ref=mix_recv.at[it, at],
-            send_sem=mix_ss.at[peer],
-            recv_sem=mix_rs.at[it, at],
+            src_ref=pair_send.at[it, peer],
+            dst_ref=pair_recv.at[it, at],
+            send_sem=pair_ss.at[peer],
+            recv_sem=pair_rs.at[it, at],
             device_id=(r, peer),
             device_id_type=MESH,
         )
 
-    def pts_copy(it, peer, at):
+    def val_copy(it, peer, at):
         return pltpu.make_async_remote_copy(
-            src_ref=pts_send.at[it, peer],
-            dst_ref=pts_recv.at[it, at],
-            send_sem=pts_ss.at[peer],
-            recv_sem=pts_rs.at[it, at],
+            src_ref=val_send.at[it, peer],
+            dst_ref=val_recv.at[it, at],
+            send_sem=val_ss.at[peer],
+            recv_sem=val_rs.at[it, at],
             device_id=(r, peer),
             device_id_type=MESH,
         )
@@ -374,15 +372,16 @@
         zeros64 = jnp.zeros((64, D), BF16)
         zeros32 = jnp.zeros((32, D), BF16)
         for part, (dst_mix, dst_loc) in enumerate(((wmix_hi, wloc_hi), (wmix_mid, wloc_mid))):
-            dst_mix[0:192] = split2(wout_f[0:192])[part]
-            dst_mix[192:256] = zeros64
             for k in range(4):
-                dst_mix[256 + 384 * k : 640 + 384 * k] = split2(
-                    wout_f[576 + 384 * k : 960 + 384 * k]
-                )[part]
+                dst_mix[384 * k : 384 * k + 384] = split2(wout_f[576 + 384 * k : 960 + 384 * k])[
+                    part
+                ]
+            dst_loc[0:192] = split2(wout_f[0:192])[part]
+            dst_loc[192:256] = zeros64
             for k in range(4):
-                dst_loc[128 * k : 128 * k + 96] = split2(wout_f[192 + 96 * k : 288 + 96 * k])[part]
-                dst_loc[128 * k + 96 : 128 * k + 128] = zeros32
+                at = 256 + 128 * k
+                dst_loc[at : at + 96] = split2(wout_f[192 + 96 * k : 288 + 96 * k])[part]
+                dst_loc[at + 96 : at + 128] = zeros32
         whid_hi[...], whid_mid[...] = split2(whid_f[...])
         wback_hi[...], wback_mid[...] = split2(wback_f[...])
         wfr_f[...] = jnp.zeros_like(wfr_f)
@@ -541,102 +540,100 @@
 
         with jax.named_scope("pack"):
             lane = lane_iota(8)
-            tops = jnp.zeros((8, 128), F32)
-            sums = jnp.zeros((8, 128), F32)
-            for g in range(8):
-                for h in range(HP):
+            for g in range(NC):
+                tile = jnp.zeros((8, 128), F32)
+                for h in range(H):
                     src = pl.ds(8 * HP * g + h, 8, stride=HP)
-                    tops = jnp.where(lane == g * HP + h, m_b[src, :], tops)
-                    sums = jnp.where(lane == g * HP + h, s_b[src, :], sums)
-            sync_send[it, 0:8] = tops
-            sync_send[it, 8:16] = sums
+                    tile = jnp.where(lane == h, m_b[src, :], tile)
+                    tile = jnp.where(lane == HP + h, s_b[src, :], tile)
+                top_send[it, g] = tile
             for peer in row_peers:
-                sync_copy(it, peer, c).start()
-            sync_recv[it, c] = sync_send[it]
-
-        with jax.named_scope("values"):
-            @pl.when(it == 0)
-            def _():
-                prepare_weights()
-
-            value_features(it)
-        with jax.named_scope("sums"):
+                top_copy(it, peer, c).start()
+        with jax.named_scope("pairs"):
             for i in range(ROWS):
                 part = pl.ds(i * HP, HP)
                 pair_s[part, :] = mm(p_s[part, 0:128], pair_v[i])
+            for h in range(H):
+                pair_send[it, :, :, 128 * h : 128 * h + 128] = (
+                    pair_s[pl.ds(h, ROWS, stride=HP), :].astype(BF16).reshape(NC, OWN, 128)
+                )
+            for peer in row_peers:
+                pair_copy(it, peer, c).start()
+        with jax.named_scope("values"):
+            value_features(it)
+        with jax.named_scope("sums"):
             values = vcat[...]
             for k in range(4):
                 part = pl.ds(k * 256, 256)
                 y = mm(p_s[part, :], values)
                 for t in range(5):
                     r_s[t, part, :] = y[:, 128 * t : 128 * t + 128]
-
-        wide = lane_iota(ROWS)
-
-        def layout_of(t):
-            if t == 0:
-                return range(0, 8), 0, C
-            if t == 1:
-                return range(8, 12), 8, C
-            return range(0, H), 0, PV
-
-        def by_head(t, piece):
-            heads, first, size = layout_of(t)
-            out = jnp.zeros((ROWS, 128), F32)
-            for h in heads:
-                lo = (h - first) * size
-                out = jnp.where((wide >= lo) & (wide < lo + size), piece(h), out)
-            return out
-
         with jax.named_scope("select"):
             for t in range(5):
-                sums_s[t] = by_head(t, lambda h: r_s[t, pl.ds(h, ROWS, stride=HP), :])
-
-        with jax.named_scope("wait_sync"):
+                val_send[it, :, :, 128 * t : 128 * t + 128] = by_head(
+                    t, ROWS, lambda h: r_s[t, pl.ds(h, ROWS, stride=HP), :]
+                ).reshape(NC, OWN, 128)
             for peer in row_peers:
-                sync_copy(it, peer, peer).wait_recv()
-        all_tops = [sync_recv[it, k, 0:8] for k in range(NC)]
-        top = functools.reduce(jnp.maximum, all_tops)
-        total = jnp.zeros((8, 128), F32)
-        for k in range(NC):
-            total = total + sync_recv[it, k, 8:16] * jnp.exp(all_tops[k] - top)
-        factor = jnp.exp(tops - top) / total
-
-        with jax.named_scope("factor"):
-            scale = []
-            for h in range(H):
-                scale.append(
-                    jnp.concatenate([column(factor, g * HP + h) for g in range(8)], axis=0)
-                )
-
-            scale_points = by_head(2, lambda h: scale[h])
-            for a in range(3):
-                pts_send[it, :, :, 128 * a : 128 * a + 128] = (sums_s[2 + a] * scale_points).reshape(
-                    NC, OWN, 128
-                )
+                val_copy(it, peer, c).start()
+            top_recv[it, c] = top_send[it, c]
+            pair_recv[it, c] = pair_send[it, c]
+            val_recv[it, c] = val_send[it, c]
+
+            @pl.when(it == 0)
+            def _():
+                prepare_weights()
+
+    def by_head(t, rows, piece):
+        if t == 0:
+            heads, first, size = range(0, 8), 0, C
+        elif t == 1:
+            heads, first, size = range(8, 12), 8, C
+        else:
+            heads, first, size = range(0, H), 0, PV
+        lane = lane_iota(rows)
+        out = jnp.zeros((rows, 128), F32)
+        for h in heads:
+            lo = (h - first) * size
+            out = jnp.where((lane >= lo) & (lane < lo + size), piece(h), out)
+        return out
+
+    def advance(it):
+        with jax.named_scope("wait_top"):
             for peer in row_peers:
-                pts_copy(it, peer, c).start()
-        with jax.named_scope("mix"):
-            pairs = [pair_s[pl.ds(h, ROWS, stride=HP), :] * scale[h] for h in range(H)]
-            scalars = [sums_s[t] * by_head(t, lambda h: scale[h]) for t in range(2)]
-            mixed_in = jnp.concatenate(scalars + pairs, axis=1)
-            mixed = dot3(mixed_in, wmix_hi[...], wmix_mid[...])
-            mix_send[it] = mixed.reshape(NC, OWN, D)
+                top_copy(it, peer, peer).wait_recv()
+        tops = [top_recv[it, k] for k in range(NC)]
+        top = functools.reduce(jnp.maximum, tops)
+        scales = [jnp.exp(t - top) for t in tops]
+        total = scales[0] * pltpu.roll(tops[0], 128 - HP, 1)
+        for k in range(1, NC):
+            total = total + scales[k] * pltpu.roll(tops[k], 128 - HP, 1)
+        inverse = 1.0 / jnp.where(lane_iota(OWN) < H, total, 1.0)
+        factor = [[column(e * inverse, h) for h in range(H)] for e in scales]
+        with jax.named_scope("wait_pair"):
             for peer in row_peers:
-                mix_copy(it, peer, c).start()
-            pts_recv[it, c] = pts_send[it, c]
-            mix_recv[it, c] = mix_send[it, c]
-
-    def advance(it):
-        with jax.named_scope("wait_pts"):
+                pair_copy(it, peer, peer).wait_recv()
+        pairs = []
+        for h in range(H):
+            at = pl.ds(128 * h, 128)
+            out = factor[0][h] * pair_recv[it, 0, :, at].astype(F32)
+            for k in range(1, NC):
+                out = out + factor[k][h] * pair_recv[it, k, :, at].astype(F32)
+            pairs.append(out)
+        mixed = dot3(jnp.concatenate(pairs, axis=1), wmix_hi[...], wmix_mid[...])
+        spread = [[by_head(t, OWN, lambda h: factor[k][h]) for t in range(3)] for k in range(NC)]
+        with jax.named_scope("wait_val"):
             for peer in row_peers:
-                pts_copy(it, peer, peer).wait_recv()
-        points = pts_recv[it, 0]
-        for k in range(1, NC):
-            points = points + pts_recv[it, k]
+                val_copy(it, peer, peer).wait_recv()
+        tiles = []
+        for t in range(5):
+            at = pl.ds(128 * t, 128)
+            out = spread[0][min(t, 2)] * val_recv[it, 0, :, at]
+            for k in range(1, NC):
+                out = out + spread[k][min(t, 2)] * val_recv[it, k, :, at]
+            tiles.append(out)
         frames = state_f[:, D:]
         single = state_f[:, :D]
-        moved = [points[:, 128 * a : 128 * a + 128] - column(frames, 9 + a) for a in range(3)]
+        moved = [tiles[2 + a] - column(frames, 9 + a) for a in range(3)]
         local = [
             column(frames, a) * moved[0]
             + column(frames, 3 + a) * moved[1]
@@ -647,13 +644,9 @@
             local[0] * local[0] + local[1] * local[1] + local[2] * local[2] + NORM_FLOOR
         )
         keep = lane_iota(OWN) < H * PV
-        feats = jnp.concatenate([jnp.where(keep, x, 0.0) for x in local + [lengths]], axis=1)
-        single = single + dot3(feats, wloc_hi[...], wloc_mid[...])
-        with jax.named_scope("wait_mix"):
-            for peer in row_peers:
-                mix_copy(it, peer, peer).wait_recv()
-        for k in range(NC):
-            single = single + mix_recv[it, k]
+        feats = tiles[:2] + [jnp.where(keep, x, 0.0) for x in local + [lengths]]
+        feats = jnp.concatenate(feats, axis=1)
+        single = single + mixed + dot3(feats, wloc_hi[...], wloc_mid[...])
         single = layer_norm(single)
         hidden = jnp.maximum(dot3(single, whid_hi[...], whid_mid[...]), 0.0)
         single = layer_norm(single + dot3(hidden, wback_hi[...], wback_mid[...]))
@@ -741,9 +734,9 @@
             swap_copy(it).wait_send()
             for peer in row_peers:
                 row_copy(it, peer, c).wait_send()
-                sync_copy(it, peer, c).wait_send()
-                pts_copy(it, peer, c).wait_send()
-                mix_copy(it, peer, c).wait_send()
+                top_copy(it, peer, c).wait_send()
+                pair_copy(it, peer, c).wait_send()
+                val_copy(it, peer, c).wait_send()
             for peer in col_peers:
                 col_copy(it, peer, slot).wait_send()
         return carry
@@ -790,10 +783,10 @@
         V((128, D), F32),
         V((D, 3 * QW), BF16),
         V((D, 3 * QW), BF16),
-        V((MIXW, D), BF16),
-        V((MIXW, D), BF16),
-        V((512, D), BF16),
-        V((512, D), BF16),
+        V((H * 128, D), BF16),
+        V((H * 128, D), BF16),
+        V((768, D), BF16),
+        V((768, D), BF16),
         V((D, D), BF16),
         V((D, D), BF16),
         V((D, D), BF16),
@@ -810,12 +803,12 @@
         V((ITERS, NC, OWN, SW), BF16),
         V((ITERS, OWN, SW), BF16),
         V((ITERS, NR, OWN, SW), BF16),
-        V((ITERS, 16, 128), F32),
-        V((ITERS, NC, 16, 128), F32),
-        V((ITERS, NC, OWN, D), F32),
-        V((ITERS, NC, OWN, D), F32),
-        V((ITERS, NC, OWN, D), F32),
-        V((ITERS, NC, OWN, D), F32),
+        V((ITERS, NC, OWN, 128), F32),
+        V((ITERS, NC, OWN, 128), F32),
+        V((ITERS, NC, OWN, H * 128), BF16),
+        V((ITERS, NC, OWN, H * 128), BF16),
+        V((ITERS, NC, OWN, QW), F32),
+        V((ITERS, NC, OWN, QW), F32),
         V((2, NC, OWN, 128), BF16),
         V((COLS, 128), F32),
         V((ROWS, FW), F32),
@@ -827,7 +820,6 @@
         V((ROWS * HP, 128), F32),
         V((ROWS * HP, 128), F32),
         V((5, ROWS * HP, 128), F32),
-        V((5, ROWS, 128), F32),
         V((ROWS * HP, 128), F32),
         dma((16,)),
         dma((NC,)),

time: 78 us -> 72.4 us (0.928)
  Pallas kernels: 77.1 us -> 71.1 us
    pallas_call x1, Pallas kernels: 75.8 us -> 69.8 us  [body(): pl.pallas_call(kernel, out_shape=(jax.ShapeDtypeStruct((OWN, D), F32), ja...]
where the time goes in v5:
time: 72.4 us; the launch traced here: 71.7 us
  Pallas kernels  71.1 us (98%)
    pallas_call x1, Pallas kernels, body(): pl.pallas_call(kernel, out_shape=(jax.ShapeDtypeStruct((OWN, D), F32), ja...  69.8 us

profile of v5, /device:TPU:0, one launch (start us, length us, event | category | flops | bytes accessed | tf_op | source)
XLA Modules:
  0.0 71.7 jit_solution(10208474575812732394)
XLA Ops:
  0.6 69.8 %structure.1 = (f32[8,384]{1,0:T(8,128)}, f32[8,12]{1,0:T(8,128)}) custom-call(f32[8,384]{1,0:T(8,128)} %single_hbm.1, f32[3,8]{1,0:T(4,128)} %rotation_hbm.1, f32[3,8]{1,0:T(4,128)} %translation_hbm.1, s32[1,8]{1,0:T(1,128)} %bitcast.13, s32[1,8]{1,0:T(1,128)} %bitcast.14, f32[1,12]{1,0:T(1,128)} %bitcast.15, bf16[128,128]{1,0:T(8,128)(2,1)} %relpos_hbm.1, ...), custom_call_target="tpu_custom_call" | custom-call | tf_op jit(solution)/shard_map/structure/pallas_call | solution.py:840
  70.4 1.3 %hand_over.1 = (f32[8,384]{1,0:T(8,128)}, f32[8,12]{1,0:T(8,128)}) custom-call(f32[8,384]{1,0:T(8,128)} %get-tuple-element.6.state, f32[8,12]{1,0:T(8,128)} %get-tuple-element.7.frames), custom_call_target="tpu_custom_call" | custom-call | tf_op jit(solution)/shard_map/hand_over/pallas_call | solution.py:859

commit v6 on v5

--- a/solution.py
+++ b/solution.py
@@ -16,6 +16,7 @@
 ITERS = 3
 D = 384
 HP = 16
+PITCH = 24
 ROWS = 64
 COLS = 128
 OWN = 8
@@ -23,6 +24,7 @@
 NC = 8
 SW = 512
 QW = 640
+VW = 512
 FW = 1024
 
 NORM_EPSILON = 1e-05
@@ -106,13 +108,13 @@
     y_hi = r // 8
     x = lax.rem(c, 4)
     y_lo = c // 4
-    to_row = y_lo * 8 + lax.rem(2 * z + 6 - x, 4) * 2 + core
+    to_row = y_lo * 8 + lax.rem(x + 2, 4) * 2 + core
     to_col = y_hi * 4 + z
     from_row = y_lo * 8 + x * 2 + core
-    from_col = y_hi * 4 + lax.rem(2 * x + 6 - z, 4)
+    from_col = y_hi * 4 + lax.rem(z + 2, 4)
 
     def slot_of(row):
-        return lax.rem(row, 2) * 8 + (row // 8) * 4 + lax.rem(2 * x + 6 - lax.rem(row // 2, 4), 4)
+        return lax.rem(row, 2) * 8 + (row // 8) * 4 + lax.rem(row // 2 + 2, 4)
 
     slot = slot_of(r)
     near = (r >= 2 * c - 1) & (r <= 2 * c + 2)
@@ -351,37 +353,36 @@
             wp_hi[:, 128 * block : 128 * block + 128] = hi
             wp_mid[:, 128 * block : 128 * block + 128] = mid
 
-        for g in range(3):
+        for g in range(2):
             at = g * H * C
             place(5 * g, wsc_f[at : at + 128])
             place(5 * g + 1, jnp.concatenate([wsc_f[at + 128 : at + 192], zeros64], axis=0))
             for a in range(3):
-                if g < 2:
-                    first = g * 144 + 48 * a
-                    part = wpt_f[first : first + 48]
-                    rows = jnp.concatenate([part, part, zeros32], axis=0)
-                else:
-                    rows = jnp.concatenate(
-                        [wpt_f[288 + 96 * a : 384 + 96 * a], zeros32], axis=0
-                    )
-                place(5 * g + 2 + a, rows)
+                first = g * 144 + 48 * a
+                part = wpt_f[first : first + 48]
+                place(5 * g + 2 + a, jnp.concatenate([part, part, zeros32], axis=0))
+        at = 2 * H * C
+        for a in range(3):
+            part = wsc_f[at + 32 * a : at + 32 * a + 32]
+            place(10 + a, jnp.concatenate([wpt_f[288 + 96 * a : 384 + 96 * a], part], axis=0))
+        place(13, jnp.concatenate([wsc_f[at + 96 : at + 192], zeros32], axis=0))
 
     def prepare_weights():
         for cp in copies[3:]:
             cp.wait()
-        zeros64 = jnp.zeros((64, D), BF16)
         zeros32 = jnp.zeros((32, D), BF16)
         for part, (dst_mix, dst_loc) in enumerate(((wmix_hi, wloc_hi), (wmix_mid, wloc_mid))):
             for k in range(4):
                 dst_mix[384 * k : 384 * k + 384] = split2(wout_f[576 + 384 * k : 960 + 384 * k])[
                     part
                 ]
-            dst_loc[0:192] = split2(wout_f[0:192])[part]
-            dst_loc[192:256] = zeros64
-            for k in range(4):
-                at = 256 + 128 * k
-                dst_loc[at : at + 96] = split2(wout_f[192 + 96 * k : 288 + 96 * k])[part]
-                dst_loc[at + 96 : at + 128] = zeros32
+            for k in range(3):
+                dst_loc[128 * k : 128 * k + 96] = split2(wout_f[192 + 96 * k : 288 + 96 * k])[part]
+                dst_loc[128 * k + 96 : 128 * k + 128] = split2(wout_f[32 * k : 32 * k + 32])[part]
+            dst_loc[384:480] = split2(wout_f[96:192])[part]
+            dst_loc[480:512] = zeros32
+            dst_loc[512:608] = split2(wout_f[480:576])[part]
+            dst_loc[608:640] = zeros32
         whid_hi[...], whid_mid[...] = split2(whid_f[...])
         wback_hi[...], wback_mid[...] = split2(wback_f[...])
         wfr_f[...] = jnp.zeros_like(wfr_f)
@@ -462,14 +463,15 @@
     def value_features(it):
         s, f = unpack(col_recv[it])
         y = mm(s, wp_hi[:, 2 * QW :]) + mm(s, wp_mid[:, 2 * QW :])
-        vcat[0:COLS, 0:256] = y[:, :256].astype(BF16)
-        vcat[COLS:, 0:256] = jnp.zeros((COLS, 256), BF16)
-        values = to_global(f, y[:, 256:], 96)
+        values = to_global(f, y, 96)
+        lane = lane_iota(COLS)
         for a in range(3):
-            hi, mid = split2(values[a])
-            at = 256 + 128 * a
+            at = 128 * a
+            hi, mid = split2(jnp.where(lane < 96, values[a], y[:, at : at + 128]))
             vcat[0:COLS, at : at + 128] = hi
-            vcat[COLS:, at : at + 128] = mid
+            vcat[COLS:, at : at + 128] = jnp.where(lane < 96, mid.astype(F32), 0.0).astype(BF16)
+        vcat[0:COLS, 384:512] = y[:, 384:512].astype(BF16)
+        vcat[COLS:, 384:512] = jnp.zeros((COLS, 128), BF16)
 
     def prepare_pair():
         copies[2].wait()
@@ -519,6 +521,10 @@
             part = pl.ds(k * 256, 256)
             bias_v[part, :] = jnp.where(live, bias_v[part, :], DEAD)
 
+    def store_queries(ref, first, rows):
+        for k in range(rows.shape[0] // HP):
+            ref[pl.ds((first + k) * PITCH, HP), :] = rows[HP * k : HP * k + HP]
+
     def attend(it):
         with jax.named_scope("logits"):
             keys = kf[...]
@@ -532,30 +538,38 @@
                 logits = jnp.where(bias > -1e38, acc * (THIRD / math.sqrt(C)) + bias, MASKED_LOGIT)
                 top = jnp.max(logits, axis=-1, keepdims=True)
                 p = jnp.exp(logits - top).astype(BF16)
-                m_b[part, :] = jnp.broadcast_to(top, (rows, 128))
+                top = jnp.broadcast_to(top, (rows, 128))
                 total = jnp.sum(p.astype(F32), axis=-1, keepdims=True)
-                s_b[part, :] = jnp.broadcast_to(total, (rows, 128))
+                total = jnp.broadcast_to(total, (rows, 128))
+                store_queries(m_b, k * rows // HP, top)
+                store_queries(s_b, k * rows // HP, total)
                 p_s[part, 0:128] = p
                 p_s[part, 128:256] = p
 
         with jax.named_scope("pack"):
             lane = lane_iota(8)
+            place = jnp.where(lane < 96, lax.rem(lane, 32), -1)
             for g in range(NC):
                 tile = jnp.zeros((8, 128), F32)
                 for h in range(H):
-                    src = pl.ds(8 * HP * g + h, 8, stride=HP)
-                    tile = jnp.where(lane == h, m_b[src, :], tile)
-                    tile = jnp.where(lane == HP + h, s_b[src, :], tile)
-                top_send[it, g] = tile
+                    src = pl.ds(8 * PITCH * g + h, 8, stride=PITCH)
+                    tile = jnp.where(place == h, m_b[src, :], tile)
+                    tile = jnp.where(place == HP + h, s_b[src, :], tile)
+                hi, mid = split2(tile)
+                lo = tile - hi.astype(F32) - mid.astype(F32)
+                tile = jnp.where(
+                    lane < 32, hi.astype(F32), jnp.where(lane < 64, mid.astype(F32), lo)
+                )
+                top_send[it, g] = tile.astype(BF16)
             for peer in row_peers:
                 top_copy(it, peer, c).start()
         with jax.named_scope("pairs"):
             for i in range(ROWS):
                 part = pl.ds(i * HP, HP)
-                pair_s[part, :] = mm(p_s[part, 0:128], pair_v[i])
+                store_queries(pair_s, i, mm(p_s[part, 0:128], pair_v[i]))
             for h in range(H):
                 pair_send[it, :, :, 128 * h : 128 * h + 128] = (
-                    pair_s[pl.ds(h, ROWS, stride=HP), :].astype(BF16).reshape(NC, OWN, 128)
+                    pair_s[pl.ds(h, ROWS, stride=PITCH), :].astype(BF16).reshape(NC, OWN, 128)
                 )
             for peer in row_peers:
                 pair_copy(it, peer, c).start()
@@ -566,12 +580,12 @@
             for k in range(4):
                 part = pl.ds(k * 256, 256)
                 y = mm(p_s[part, :], values)
-                for t in range(5):
-                    r_s[t, part, :] = y[:, 128 * t : 128 * t + 128]
+                for t in range(4):
+                    store_queries(r_s.at[t], 16 * k, y[:, 128 * t : 128 * t + 128])
         with jax.named_scope("select"):
-            for t in range(5):
+            for t in range(4):
                 val_send[it, :, :, 128 * t : 128 * t + 128] = by_head(
-                    t, ROWS, lambda h: r_s[t, pl.ds(h, ROWS, stride=HP), :]
+                    t, ROWS, lambda h: r_s[t, pl.ds(h, ROWS, stride=PITCH), :]
                 ).reshape(NC, OWN, 128)
             for peer in row_peers:
                 val_copy(it, peer, c).start()
@@ -584,16 +598,12 @@
                 prepare_weights()
 
     def by_head(t, rows, piece):
-        if t == 0:
-            heads, first, size = range(0, 8), 0, C
-        elif t == 1:
-            heads, first, size = range(8, 12), 8, C
-        else:
-            heads, first, size = range(0, H), 0, PV
+        spans = [(h, PV * h, PV) for h in range(H)] if t < 3 else []
+        at, heads = (96, range(2 * t, 2 * t + 2)) if t < 3 else (0, range(6, H))
+        spans += [(h, at + C * (h - heads[0]), C) for h in heads]
         lane = lane_iota(rows)
         out = jnp.zeros((rows, 128), F32)
-        for h in heads:
-            lo = (h - first) * size
+        for h, lo, size in spans:
             out = jnp.where((lane >= lo) & (lane < lo + size), piece(h), out)
         return out
 
@@ -601,7 +611,10 @@
         with jax.named_scope("wait_top"):
             for peer in row_peers:
                 top_copy(it, peer, peer).wait_recv()
-        tops = [top_recv[it, k] for k in range(NC)]
+        tops = []
+        for k in range(NC):
+            tile = top_recv[it, k].astype(F32)
+            tops.append(tile + pltpu.roll(tile, 96, 1) + pltpu.roll(tile, 64, 1))
         top = functools.reduce(jnp.maximum, tops)
         scales = [jnp.exp(t - top) for t in tops]
         total = scales[0] * pltpu.roll(tops[0], 128 - HP, 1)
@@ -620,20 +633,20 @@
                 out = out + factor[k][h] * pair_recv[it, k, :, at].astype(F32)
             pairs.append(out)
         mixed = dot3(jnp.concatenate(pairs, axis=1), wmix_hi[...], wmix_mid[...])
-        spread = [[by_head(t, OWN, lambda h: factor[k][h]) for t in range(3)] for k in range(NC)]
+        spread = [[by_head(t, OWN, lambda h: factor[k][h]) for t in range(4)] for k in range(NC)]
         with jax.named_scope("wait_val"):
             for peer in row_peers:
                 val_copy(it, peer, peer).wait_recv()
         tiles = []
-        for t in range(5):
+        for t in range(4):
             at = pl.ds(128 * t, 128)
-            out = spread[0][min(t, 2)] * val_recv[it, 0, :, at]
+            out = spread[0][t] * val_recv[it, 0, :, at]
             for k in range(1, NC):
-                out = out + spread[k][min(t, 2)] * val_recv[it, k, :, at]
+                out = out + spread[k][t] * val_recv[it, k, :, at]
             tiles.append(out)
         frames = state_f[:, D:]
         single = state_f[:, :D]
-        moved = [tiles[2 + a] - column(frames, 9 + a) for a in range(3)]
+        moved = [tiles[a] - column(frames, 9 + a) for a in range(3)]
         local = [
             column(frames, a) * moved[0]
             + column(frames, 3 + a) * moved[1]
@@ -644,7 +657,8 @@
             local[0] * local[0] + local[1] * local[1] + local[2] * local[2] + NORM_FLOOR
         )
         keep = lane_iota(OWN) < H * PV
-        feats = tiles[:2] + [jnp.where(keep, x, 0.0) for x in local + [lengths]]
+        feats = [jnp.where(keep, local[a], tiles[a]) for a in range(3)]
+        feats += [tiles[3], jnp.where(keep, lengths, 0.0)]
         feats = jnp.concatenate(feats, axis=1)
         single = single + mixed + dot3(feats, wloc_hi[...], wloc_mid[...])
         single = layer_norm(single)
@@ -781,12 +795,12 @@
         V((D, D), F32),
         V((D, D), F32),
         V((128, D), F32),
-        V((D, 3 * QW), BF16),
-        V((D, 3 * QW), BF16),
+        V((D, 2 * QW + VW), BF16),
+        V((D, 2 * QW + VW), BF16),
         V((H * 128, D), BF16),
         V((H * 128, D), BF16),
-        V((768, D), BF16),
-        V((768, D), BF16),
+        V((QW, D), BF16),
+        V((QW, D), BF16),
         V((D, D), BF16),
         V((D, D), BF16),
         V((D, D), BF16),
@@ -803,24 +817,24 @@
         V((ITERS, NC, OWN, SW), BF16),
         V((ITERS, OWN, SW), BF16),
         V((ITERS, NR, OWN, SW), BF16),
-        V((ITERS, NC, OWN, 128), F32),
-        V((ITERS, NC, OWN, 128), F32),
+        V((ITERS, NC, OWN, 128), BF16),
+        V((ITERS, NC, OWN, 128), BF16),
         V((ITERS, NC, OWN, H * 128), BF16),
         V((ITERS, NC, OWN, H * 128), BF16),
-        V((ITERS, NC, OWN, QW), F32),
-        V((ITERS, NC, OWN, QW), F32),
+        V((ITERS, NC, OWN, VW), F32),
+        V((ITERS, NC, OWN, VW), F32),
         V((2, NC, OWN, 128), BF16),
         V((COLS, 128), F32),
         V((ROWS, FW), F32),
         V((ROWS * HP, FW), BF16),
         V((COLS, FW), BF16),
-        V((2 * COLS, QW), BF16),
+        V((2 * COLS, VW), BF16),
         V((2 * ROWS, 128), F32),
         V((ROWS * HP, 256), BF16),
-        V((ROWS * HP, 128), F32),
-        V((ROWS * HP, 128), F32),
-        V((5, ROWS * HP, 128), F32),
-        V((ROWS * HP, 128), F32),
+        V((ROWS * PITCH, 128), F32),
+        V((ROWS * PITCH, 128), F32),
+        V((4, ROWS * PITCH, 128), F32),
+        V((ROWS * PITCH, 128), F32),
         dma((16,)),
         dma((NC,)),
         dma((ITERS, NC)),

time: 72.4 us -> 71.6 us (0.989)
  Pallas kernels: 71.1 us -> 70.3 us
    pallas_call x1, Pallas kernels: 69.8 us -> 69 us  [body(): pl.pallas_call(kernel, out_shape=(jax.ShapeDtypeStruct((OWN, D), F32), ja...]
where the time goes in v6:
time: 71.6 us; the launch traced here: 70.9 us
  Pallas kernels  70.3 us (98%)
    pallas_call x1, Pallas kernels, body(): pl.pallas_call(kernel, out_shape=(jax.ShapeDtypeStruct((OWN, D), F32), ja...  69 us

profile of v6, /device:TPU:0, one launch (start us, length us, event | category | flops | bytes accessed | tf_op | source)
XLA Modules:
  0.0 70.9 jit_solution(13834610092029474341)
XLA Ops:
  0.6 69.0 %structure.1 = (f32[8,384]{1,0:T(8,128)}, f32[8,12]{1,0:T(8,128)}) custom-call(f32[8,384]{1,0:T(8,128)} %single_hbm.1, f32[3,8]{1,0:T(4,128)} %rotation_hbm.1, f32[3,8]{1,0:T(4,128)} %translation_hbm.1, s32[1,8]{1,0:T(1,128)} %bitcast.13, s32[1,8]{1,0:T(1,128)} %bitcast.14, f32[1,12]{1,0:T(1,128)} %bitcast.15, bf16[128,128]{1,0:T(8,128)(2,1)} %relpos_hbm.1, ...), custom_call_target="tpu_custom_call" | custom-call | tf_op jit(solution)/shard_map/structure/pallas_call | solution.py:854
  69.6 1.3 %hand_over.1 = (f32[8,384]{1,0:T(8,128)}, f32[8,12]{1,0:T(8,128)}) custom-call(f32[8,384]{1,0:T(8,128)} %get-tuple-element.6.state, f32[8,12]{1,0:T(8,128)} %get-tuple-element.7.frames), custom_call_target="tpu_custom_call" | custom-call | tf_op jit(solution)/shard_map/hand_over/pallas_call | solution.py:873

commit v7 on v6

--- a/solution.py
+++ b/solution.py
@@ -99,7 +99,7 @@
     val_send, val_recv, idx_recv, key_idx,
     qf, qmask, kf, vcat, idx_b, p_s, m_b, s_b, r_s, pair_s,
     copy_sem, row_ss, row_rs, swap_ss, swap_rs, col_ss, col_rs, top_ss, top_rs,
-    pair_ss, pair_rs, val_ss, val_rs, idx_ss, idx_rs,
+    pair_ss, pair_rs, val_ss, val_rs, idx_ss, idx_rs, far_ss,
 ):
     r = lax.axis_index("row")
     c = lax.axis_index("col")
@@ -113,6 +113,9 @@
     from_row = y_lo * 8 + x * 2 + core
     from_col = y_hi * 4 + lax.rem(z + 2, 4)
 
+    far_rows = [(1 - y_lo) * 8 + x * 2 + k for k in (0, 1)]
+    far_sources = [(y_lo * 8 + x * 2 + k, (1 - y_hi) * 4 + z) for k in (0, 1)]
+
     def slot_of(row):
         return lax.rem(row, 2) * 8 + (row // 8) * 4 + lax.rem(row // 2 + 2, 4)
 
@@ -130,6 +133,7 @@
         for dc in (0, 1)
         if (dy, dz, dc) != (0, 0, 0)
     ]
+    served = col_peers[2:]
 
     barrier = pltpu.get_barrier_semaphore()
     for peer in col_peers:
@@ -137,6 +141,8 @@
     for peer in row_peers:
         pl.semaphore_signal(barrier, inc=1, device_id=(r, peer), device_id_type=MESH)
     pl.semaphore_signal(barrier, inc=1, device_id=(from_row, from_col), device_id_type=MESH)
+    for peer in far_sources:
+        pl.semaphore_signal(barrier, inc=1, device_id=peer, device_id_type=MESH)
 
     small_copies = [
         pltpu.make_async_copy(src, dst, copy_sem.at[6 + k])
@@ -223,7 +229,7 @@
         hmask[:, 128 * t : 128 * t + 128] = jnp.where(own & (head_row < H), 1.0, 0.0)
 
     with jax.named_scope("barrier"):
-        pl.semaphore_wait(barrier, NC + NR - 1)
+        pl.semaphore_wait(barrier, NC + NR + 1)
 
     def row_copy(it, peer, at):
         return pltpu.make_async_remote_copy(
@@ -245,6 +251,16 @@
             device_id_type=MESH,
         )
 
+    def far_copy(it, k, at):
+        return pltpu.make_async_remote_copy(
+            src_ref=send_buf.at[it],
+            dst_ref=col_recv.at[it, at],
+            send_sem=far_ss.at[k],
+            recv_sem=col_rs.at[it, at],
+            device_id=(far_rows[k], to_col),
+            device_id_type=MESH,
+        )
+
     def col_copy(it, peer, at):
         return pltpu.make_async_remote_copy(
             src_ref=swap_recv.at[it],
@@ -338,6 +354,8 @@
 
     def start_exchange(it):
         swap_copy(it).start()
+        for k in (0, 1):
+            far_copy(it, k, core * 8 + c).start()
         for peer in row_peers:
             row_copy(it, peer, c).start()
         row_recv[it, c] = send_buf[it]
@@ -698,7 +716,7 @@
         with jax.named_scope("wait_swap"):
             swap_copy(it).wait_recv()
         with jax.named_scope("send_col"):
-            for peer in col_peers:
+            for peer in served:
                 col_copy(it, peer, slot).start()
             col_recv[it, slot] = swap_recv[it]
 
@@ -720,8 +738,10 @@
                 prepare_pair()
 
         with jax.named_scope("wait_col"):
-            for peer in col_peers:
+            for peer in served:
                 col_copy(it, peer, slot_of(peer)).wait_recv()
+            for k in (0, 1):
+                far_copy(it, k, k * 8 + far_sources[k][1]).wait_recv()
         with jax.named_scope("key"):
             key_features(it)
 
@@ -751,8 +771,10 @@
                 top_copy(it, peer, c).wait_send()
                 pair_copy(it, peer, c).wait_send()
                 val_copy(it, peer, c).wait_send()
-            for peer in col_peers:
+            for peer in served:
                 col_copy(it, peer, slot).wait_send()
+            for k in (0, 1):
+                far_copy(it, k, core * 8 + c).wait_send()
         return carry
 
     lax.fori_loop(0, ITERS, iteration, 0)
@@ -850,6 +872,7 @@
         dma((ITERS, NC)),
         dma((3,)),
         dma((2,)),
+        dma((2,)),
     ]
     state, frames = pl.pallas_call(
         kernel,

time: 71.6 us -> 71.4 us (level)
  no operation moved by 1% of the time
where the time goes in v7:
time: 71.4 us; the launch traced here: 70.5 us
  Pallas kernels  69.9 us (98%)
    pallas_call x1, Pallas kernels, body(): pl.pallas_call(kernel, out_shape=(jax.ShapeDtypeStruct((OWN, D), F32), ja...  68.6 us

profile of v7, /device:TPU:0, one launch (start us, length us, event | category | flops | bytes accessed | tf_op | source)
XLA Modules:
  0.0 70.5 jit_solution(16998808310410603114)
XLA Ops:
  0.6 68.6 %structure.1 = (f32[8,384]{1,0:T(8,128)}, f32[8,12]{1,0:T(8,128)}) custom-call(f32[8,384]{1,0:T(8,128)} %single_hbm.1, f32[3,8]{1,0:T(4,128)} %rotation_hbm.1, f32[3,8]{1,0:T(4,128)} %translation_hbm.1, s32[1,8]{1,0:T(1,128)} %bitcast.13, s32[1,8]{1,0:T(1,128)} %bitcast.14, f32[1,12]{1,0:T(1,128)} %bitcast.15, bf16[128,128]{1,0:T(8,128)(2,1)} %relpos_hbm.1, ...), custom_call_target="tpu_custom_call" | custom-call | tf_op jit(solution)/shard_map/structure/pallas_call | solution.py:877
  69.2 1.3 %hand_over.1 = (f32[8,384]{1,0:T(8,128)}, f32[8,12]{1,0:T(8,128)}) custom-call(f32[8,384]{1,0:T(8,128)} %get-tuple-element.6.state, f32[8,12]{1,0:T(8,128)} %get-tuple-element.7.frames), custom_call_target="tpu_custom_call" | custom-call | tf_op jit(solution)/shard_map/hand_over/pallas_call | solution.py:896

commit v8 on v7

--- a/solution.py
+++ b/solution.py
@@ -519,16 +519,22 @@
                 onehot = jnp.where(offset == lane, 1.0, 0.0).astype(BF16)
                 both = jnp.concatenate([pair_v[first + u], onehot, onehot], axis=1)
                 centres.append(mm(both, centre[...]))
+            normed = []
             for u in range(step):
                 spread = jnp.mean(centres[u] * centres[u], axis=-1, keepdims=True)
-                normed = (centres[u] * lax.rsqrt(spread + NORM_EPSILON) * gains).astype(BF16)
-                pair_v[first + u] = normed
+                normed.append((centres[u] * lax.rsqrt(spread + NORM_EPSILON) * gains).astype(BF16))
+                pair_v[first + u] = normed[u]
+            for u in range(0, step, 2):
+                two = jnp.concatenate(normed[u : u + 2], axis=0)
                 bias = lax.dot_general(
-                    project, normed, (((1,), (1,)), ((), ())), preferred_element_type=F32
+                    project, two, (((1,), (1,)), ((), ())), preferred_element_type=F32
                 )
-                live = idx_b[pl.ds(ROWS + first + u, 1), :] > 0.5
-                at = pl.multiple_of((first + u) * HP, HP)
-                bias_v[pl.ds(at, HP), :] = jnp.where(live, bias * THIRD, DEAD)
+                for v in range(2):
+                    live = idx_b[pl.ds(ROWS + first + u + v, 1), :] > 0.5
+                    at = pl.multiple_of((first + u + v) * HP, HP)
+                    bias_v[pl.ds(at, HP), :] = jnp.where(
+                        live, bias[:, 128 * v : 128 * v + 128] * THIRD, DEAD
+                    )
             return carry
 
         lax.fori_loop(0, ROWS // step, prepare, 0)
@@ -582,9 +588,12 @@
             for peer in row_peers:
                 top_copy(it, peer, c).start()
         with jax.named_scope("pairs"):
-            for i in range(ROWS):
-                part = pl.ds(i * HP, HP)
-                store_queries(pair_s, i, mm(p_s[part, 0:128], pair_v[i]))
+            for i in range(0, ROWS, 2):
+                part = pl.ds(i * HP, 2 * HP)
+                two = jnp.concatenate([pair_v[i], pair_v[i + 1]], axis=1)
+                y = mm(p_s[part, 0:128], two)
+                store_queries(pair_s, i, y[0:HP, 0:128])
+                store_queries(pair_s, i + 1, y[HP:, 128:256])
             for h in range(H):
                 pair_send[it, :, :, 128 * h : 128 * h + 128] = (
                     pair_s[pl.ds(h, ROWS, stride=PITCH), :].astype(BF16).reshape(NC, OWN, 128)

time: 71.4 us -> 70.8 us (level)
  no operation moved by 1% of the time
where the time goes in v8:
time: 70.8 us; the launch traced here: 70 us
  Pallas kernels  69.4 us (98%)
    pallas_call x1, Pallas kernels, body(): pl.pallas_call(kernel, out_shape=(jax.ShapeDtypeStruct((OWN, D), F32), ja...  68.1 us

profile of v8, /device:TPU:0, one launch (start us, length us, event | category | flops | bytes accessed | tf_op | source)
XLA Modules:
  0.0 70.0 jit_solution(10532048299584808682)
XLA Ops:
  0.6 68.1 %structure.1 = (f32[8,384]{1,0:T(8,128)}, f32[8,12]{1,0:T(8,128)}) custom-call(f32[8,384]{1,0:T(8,128)} %single_hbm.1, f32[3,8]{1,0:T(4,128)} %rotation_hbm.1, f32[3,8]{1,0:T(4,128)} %translation_hbm.1, s32[1,8]{1,0:T(1,128)} %bitcast.13, s32[1,8]{1,0:T(1,128)} %bitcast.14, f32[1,12]{1,0:T(1,128)} %bitcast.15, bf16[128,128]{1,0:T(8,128)(2,1)} %relpos_hbm.1, ...), custom_call_target="tpu_custom_call" | custom-call | tf_op jit(solution)/shard_map/structure/pallas_call | solution.py:886
  68.7 1.3 %hand_over.1 = (f32[8,384]{1,0:T(8,128)}, f32[8,12]{1,0:T(8,128)}) custom-call(f32[8,384]{1,0:T(8,128)} %get-tuple-element.6.state, f32[8,12]{1,0:T(8,128)} %get-tuple-element.7.frames), custom_call_target="tpu_custom_call" | custom-call | tf_op jit(solution)/shard_map/hand_over/pallas_call | solution.py:905

commit v9 on v8

--- a/solution.py
+++ b/solution.py
@@ -509,7 +509,7 @@
         wb_s[0:H] = wb_in[...].astype(F32)
         project = wb_s[...].astype(BF16)
         gains = gain[...]
-        step = 8
+        step = 16
 
         def prepare(k, carry):
             first = k * step

time: 70.8 us -> 69 us (0.975)
  Pallas kernels: 69.4 us -> 67.8 us
    pallas_call x1, Pallas kernels: 68.1 us -> 66.5 us  [body(): pl.pallas_call(kernel, out_shape=(jax.ShapeDtypeStruct((OWN, D), F32), ja...]
where the time goes in v9:
time: 69 us; the launch traced here: 68.5 us
  Pallas kernels  67.8 us (98%)
    pallas_call x1, Pallas kernels, body(): pl.pallas_call(kernel, out_shape=(jax.ShapeDtypeStruct((OWN, D), F32), ja...  66.5 us

profile of v9, /device:TPU:0, one launch (start us, length us, event | category | flops | bytes accessed | tf_op | source)
XLA Modules:
  0.0 68.5 jit_solution(18056348546671293484)
XLA Ops:
  0.6 66.5 %structure.1 = (f32[8,384]{1,0:T(8,128)}, f32[8,12]{1,0:T(8,128)}) custom-call(f32[8,384]{1,0:T(8,128)} %single_hbm.1, f32[3,8]{1,0:T(4,128)} %rotation_hbm.1, f32[3,8]{1,0:T(4,128)} %translation_hbm.1, s32[1,8]{1,0:T(1,128)} %bitcast.13, s32[1,8]{1,0:T(1,128)} %bitcast.14, f32[1,12]{1,0:T(1,128)} %bitcast.15, bf16[128,128]{1,0:T(8,128)(2,1)} %relpos_hbm.1, ...), custom_call_target="tpu_custom_call" | custom-call | tf_op jit(solution)/shard_map/structure/pallas_call | solution.py:886
  67.2 1.3 %hand_over.1 = (f32[8,384]{1,0:T(8,128)}, f32[8,12]{1,0:T(8,128)}) custom-call(f32[8,384]{1,0:T(8,128)} %get-tuple-element.6.state, f32[8,12]{1,0:T(8,128)} %get-tuple-element.7.frames), custom_call_target="tpu_custom_call" | custom-call | tf_op jit(solution)/shard_map/hand_over/pallas_call | solution.py:905
